TPU v7x, 32 devices: a whole 2x2x4 slice. The times are simulated.
32 devices in a mesh: fluid: 8 (over z, x), solid: 4 (over y, core).
Axes of the slice: x: 2, y: 2, z: 4, core: 2. Of those that a mesh axis runs over, the one named last changes fastest.
Arguments:
- flow: bfloat16 [3, 262144, 128], P(None, ('fluid', 'solid')), may hold values from -6 to 6
- wall_motion: float32 [3, 262144], P(None, ('fluid', 'solid')), may hold values from -6 to 6
- normal_operator: bfloat16 [128, 128], replicated, may hold values from -0.5 to 0.5
- wall_coupling: float32 [128], replicated, may hold values from -4 to 4
- wall_stencil: bfloat16 [128], replicated, may hold values from -0.5 to 0.5
- rbf_blocks: bfloat16 [2048, 128, 128], P(('fluid', 'solid')), may hold values from -0.5 to 0.5
- block_owner: int32 [2048, 1], P(('fluid', 'solid')), may hold values from 0 to 7; in each aligned block of 64 rows (0 to 63, 64 to 127, ...) at most 12 rows name the same one
- block_row: int32 [2048, 1], P(('fluid', 'solid')), may hold values from 0 to 31
- displacement: float32 [1024, 3, 128], P(('fluid', 'solid')), may hold values from -6 to 6
- stiffness: float32 [1024, 128], P(('fluid', 'solid')), may hold values from 0.5 to 4
- residual_history: float32 [64, 1024, 3, 128], P(None, ('fluid', 'solid')), may hold values from -0.076546554 to 0.076546554
- solution_history: float32 [64, 1024, 3, 128], P(None, ('fluid', 'solid')), may hold values from -6 to 6
Outputs:
- new_flow: bfloat16 [3, 262144, 128], P(None, ('fluid', 'solid'))
- next_displacement: float32 [1024, 3, 128], P(('fluid', 'solid'))
- wall_next: float32 [3, 262144], P(None, ('fluid', 'solid'))
- residual_norm: float32 [], replicated
Inputs may be any that keep to these rules, and one draw needn't show every extreme that they name: `block_owner`: each device's 64 blocks name no owner more than 12 times, a bound that some block reaches; every owner gets some block.
All inputs are finite; a program needn't handle non-finite values.
Results may differ from a plain program's by a relative error of at most 0.0035.
The roundings to bfloat16 on the way count: a program that leaves them out, or rounds other values in their place, can miss the bound.
Values may be sent and summed in bfloat16 or wider, within the bound.
No kernel may reach another device: no remote copies, remote signals or barrier semaphores. Data moves between devices by JAX's collectives and lax.ppermute only.
A program may use at most 128 MiB of HBM per device.

v0:
```python
import jax
import jax.numpy as jnp
from jax import lax
from jax.sharding import PartitionSpec as P

SWEEPS = 4


spread_rate = 0.25


def with_halo(cells, sides, width):
    for axis, dim in sides:
        count = lax.axis_size(axis)
        ends = count - 1
        head = lax.slice_in_dim(cells, 0, width, axis=dim)
        tail = lax.slice_in_dim(cells, cells.shape[dim] - width, cells.shape[dim], axis=dim)
        cells = jnp.concatenate(
            [
                lax.ppermute(tail, axis, [(i, (i + 1) % count) for i in range(ends)]),
                cells,
                lax.ppermute(head, axis, [((i + 1) % count, i) for i in range(ends)]),
            ],
            axis=dim,
        )
    return cells


def per_device(
    flow,
    wall_motion,
    normal_operator,
    wall_coupling,
    wall_stencil,
    rbf_blocks,
    block_owner,
    block_row,
    displacement,
    stiffness,
    residual_history,
    solution_history,
):
    groups = lax.axis_size("fluid")
    comps, points, normal = flow.shape
    padded = with_halo(flow, ((("fluid", "solid"), 1),), 1)
    field = flow.astype(jnp.float32)
    drift = jnp.dot(
        flow.reshape(-1, normal), normal_operator, preferred_element_type=jnp.float32
    ).reshape(field.shape)
    spread = (
        padded[:, 2:, :].astype(jnp.float32) + padded[:, :-2, :].astype(jnp.float32) - 2.0 * field
    )
    new_flow = (
        field
        + drift
        + spread_rate * spread
        + wall_motion[:, :, None] * wall_coupling[None, None, :]
    ).astype(jnp.bfloat16)
    traction = jnp.dot(
        new_flow.reshape(-1, normal), wall_stencil, preferred_element_type=jnp.float32
    ).astype(jnp.bfloat16)
    blocks, block, width = rbf_blocks.shape
    pieces = traction.reshape(comps, blocks, block)
    mapped = jnp.einsum(
        "cbp,bpq->bcq", pieces, rbf_blocks, preferred_element_type=jnp.float32
    ).reshape(blocks, comps * width)
    rows_dev = displacement.shape[0]
    owner = block_owner[:, 0]
    local_row = block_row[:, 0]
    capacity = max(2, (3 * blocks + 2 * groups - 1) // (2 * groups))
    order = jnp.arange(blocks, dtype=jnp.int32)
    earlier = jnp.sum(
        (owner[None, :] == owner[:, None]) & (order[None, :] < order[:, None]), axis=1
    )
    slot = owner * capacity + earlier
    slots = groups * capacity
    chosen = slot[None, :] == jnp.arange(slots, dtype=jnp.int32)[:, None]
    outgoing = jnp.dot(
        chosen.astype(jnp.float32),
        mapped,
        precision=lax.Precision.HIGHEST,
        preferred_element_type=jnp.float32,
    )
    labels = jnp.sum(jnp.where(chosen, local_row[None, :] + 1, 0), axis=1)
    arrived, arrived_rows = (
        lax.all_to_all(outgoing, "fluid", split_axis=0, concat_axis=0, tiled=True),
        lax.all_to_all(labels, "fluid", split_axis=0, concat_axis=0, tiled=True),
    )
    placed = arrived_rows[None, :] == jnp.arange(rows_dev, dtype=jnp.int32)[:, None] + 1
    force = jnp.dot(
        placed.astype(jnp.float32),
        arrived,
        precision=lax.Precision.HIGHEST,
        preferred_element_type=jnp.float32,
    ).reshape(rows_dev, comps, width)
    solved = displacement
    denom = 4.0 + stiffness[:, None, :]
    for sweep in range(SWEEPS):
        rim = with_halo(solved.astype(jnp.bfloat16), ((("fluid", "solid"), 0),), 1).astype(
            solved.dtype
        )
        across = jnp.pad(solved, ((0, 0), (0, 0), (1, 1)))
        beside = rim[2:] + rim[:-2] + across[:, :, 2:] + across[:, :, :-2]
        solved = (force + beside) / denom
    residual = solved - displacement
    history = residual_history.shape[0]
    flat_res = residual_history.reshape(history, -1)
    flat = residual.reshape(-1)
    gram, proj, squares = lax.psum(
        (
            jnp.dot(flat_res, flat_res.T, precision=lax.Precision.HIGHEST),
            jnp.dot(flat_res, flat, precision=lax.Precision.HIGHEST),
            jnp.sum(flat * flat),
        ),
        ("fluid", "solid"),
    )
    lower = jnp.linalg.cholesky(gram)
    coeff = jax.scipy.linalg.cho_solve((lower, True), -proj)
    update = jnp.dot(
        coeff, solution_history.reshape(history, -1), precision=lax.Precision.HIGHEST
    ).reshape(solved.shape)
    next_displacement = solved + update
    shell = next_displacement.astype(jnp.bfloat16)
    reply = jnp.dot(
        placed.T.astype(jnp.bfloat16),
        shell.reshape(rows_dev, -1),
        preferred_element_type=jnp.float32,
    ).astype(jnp.bfloat16)
    returned = lax.all_to_all(reply, "fluid", split_axis=0, concat_axis=0, tiled=True)
    fetched = jnp.dot(chosen.T.astype(jnp.bfloat16), returned, preferred_element_type=jnp.float32)
    local = fetched.astype(jnp.bfloat16).reshape(blocks, comps, width)
    wall_next = jnp.einsum(
        "bpq,bcq->cbp", rbf_blocks, local, preferred_element_type=jnp.float32
    ).reshape(comps, blocks * block)
    return (new_flow, next_displacement, wall_next, jnp.sqrt(squares))


def solution(mesh):
    return jax.shard_map(
        per_device,
        mesh=mesh,
        in_specs=(
            P(None, ("fluid", "solid"), None),
            P(None, ("fluid", "solid")),
            P(),
            P(),
            P(),
            P(("fluid", "solid"), None, None),
            P(("fluid", "solid"), None),
            P(("fluid", "solid"), None),
            P(("fluid", "solid"), None, None),
            P(("fluid", "solid"), None),
            P(None, ("fluid", "solid"), None, None),
            P(None, ("fluid", "solid"), None, None),
        ),
        out_specs=(
            P(None, ("fluid", "solid"), None),
            P(("fluid", "solid"), None, None),
            P(None, ("fluid", "solid")),
            P(),
        ),
        check_vma=False,
    )
```

profile of v0, /device:TPU:0, one launch (start us, length us, event | category | flops | bytes accessed | tf_op | source)
XLA Modules:
  0.0 190.9 jit_solution(13724637750576522882)
XLA Ops:
  0.6 0.8 add_bitcast_fusion
  1.5 0.9 convert_reduce_fusion
  2.4 0.7 multiply_add_fusion.1
  3.1 0.7 all_to_all.20
  3.8 7.3 %all-to-all-start = ((s32[8,12,1]{1,2,0:T(1,128)}), s32[8,12,1]{1,2,0:T(1,128)S(1)}, u32[]{:S(2)}, u32[]{:S(2)}) async-start(s32[8,12,1]{1,2,0:T(1,128)} %bitcast.3), calls=%async_computation | async-start | bytes 8192 | tf_op jit(solution)/shard_map/all_to_all | solution.py:87
  11.1 0.7 fusion.71
  11.8 1.3 collective-permute-start
  13.1 3.0 %collective-permute-start.1 = (bf16[3,1,128]{2,1,0:T(2,128)(2,1)S(1)}, bf16[3,1,128]{2,1,0:T(2,128)(2,1)S(1)}, u32[]{:S(2)}, u32[]{:S(2)}) collective-permute-start(bf16[3,1,128]{2,1,0:T(2,128)(2,1)S(1)} %get-tuple-element.18), channel_id=1, source_target_pairs={{0,1},{1,2},{2,3},{3,4},{4,5},{5,6},{6,7},{7,8},{8,9},{9,10},{10,1... | collective-permute-start | bytes 2312 | tf_op jit(solution)/shard_map/ppermute | solution.py:20
  16.1 0.8 convert_element_type.66
  16.9 3.0 %collective-permute-start.2 = (bf16[1,3,128]{2,0,1:T(2,128)(2,1)S(1)}, bf16[1,3,128]{2,0,1:T(2,128)(2,1)S(1)}, u32[]{:S(2)}, u32[]{:S(2)}) collective-permute-start(bf16[1,3,128]{2,0,1:T(2,128)(2,1)S(1)} %get-tuple-element.25), channel_id=1, source_target_pairs={{0,1},{1,2},{2,3},{3,4},{4,5},{5,6},{6,7},{7,8},{8,9},{9,10},{10,1... | collective-permute-start | bytes 2312 | tf_op jit(solution)/shard_map/ppermute | solution.py:20
  20.0 1.3 collective-permute-start.3
  21.3 16.1 %fusion.2 = bf16[3,8192,128]{2,1,0:T(8,128)(2,1)S(1)} fusion(bf16[3,8192,128]{2,1,0:T(8,128)(2,1)} %param.12, bf16[3,1,128]{2,1,0:T(2,128)(2,1)S(1)} %collective-permute-done.1, bf16[3,1,128]{2,1,0:T(2,128)(2,1)S(1)} %collective-permute-done, f32[128]{0:T(128)} %param.15, f32[3,8192]{1,0:T(4,128)} %param.13, bf16[128,128]{1,0:T(8,128)(2,1)} %param.14), kind=kOutput, calls=%fused_computation.4 | convolution fusion | flops 861929472 | bytes 12716032 | tf_op jit(solution)/shard_map/dot_general | solution.py:47
  37.5 2.7 %copy-done.1 = bf16[3,8192,128]{2,1,0:T(8,128)(2,1)} copy-done((bf16[3,8192,128]{2,1,0:T(8,128)(2,1)}, bf16[3,8192,128]{2,1,0:T(8,128)(2,1)S(1)}, u32[]{:S(2)}) %copy-start.1) | copy-done | bytes 6291480
  40.2 1.7 fusion.61
  41.9 0.6 fusion.20
  42.7 1.0 fusion.22
  43.6 8.9 %all-to-all-start.1 = ((f32[8,12,384]{2,1,0:T(8,128)}), f32[8,12,384]{2,1,0:T(8,128)S(1)}, u32[]{:S(2)}, u32[]{:S(2)}) async-start(f32[8,12,384]{2,1,0:T(8,128)} %fusion.22), calls=%async_computation.1 | async-start | bytes 393216 | tf_op jit(solution)/shard_map/all_to_all | solution.py:86
  52.6 0.5 broadcast.120
  53.1 0.7 reduce.10
  53.9 6.5 %all-to-all-done.1 = f32[8,12,384]{2,1,0:T(8,128)S(1)} async-done(((f32[8,12,384]{2,1,0:T(8,128)}), f32[8,12,384]{2,1,0:T(8,128)S(1)}, u32[]{:S(2)}, u32[]{:S(2)}) %all-to-all-start.1) | async-done | bytes 147488 | tf_op jit(solution)/shard_map/all_to_all | solution.py:86
  60.4 0.2 fusion.69
  60.6 1.4 collective-permute-start.4
  62.0 1.3 collective-permute-start.5
  63.4 2.3 %collective-permute-done.5 = bf16[1,3,128]{2,0,1:T(2,128)(2,1)S(1)} collective-permute-done((bf16[1,3,128]{2,0,1:T(2,128)(2,1)S(1)}, bf16[1,3,128]{2,0,1:T(2,128)(2,1)S(1)}, u32[]{:S(2)}, u32[]{:S(2)}) %collective-permute-start.5) | collective-permute-done | bytes 800 | tf_op jit(solution)/shard_map/ppermute | solution.py:22
  65.8 4.2 %collective-permute-start.6 = (bf16[1,3,128]{2,0,1:T(2,128)(2,1)S(1)}, bf16[1,3,128]{2,0,1:T(2,128)(2,1)S(1)}, u32[]{:S(2)}, u32[]{:S(2)}) collective-permute-start(bf16[1,3,128]{2,0,1:T(2,128)(2,1)S(1)} %get-tuple-element.21), channel_id=1, source_target_pairs={{0,1},{1,2},{2,3},{3,4},{4,5},{5,6},{6,7},{7,8},{8,9},{9,10},{10,1... | collective-permute-start | bytes 2312 | tf_op jit(solution)/shard_map/ppermute | solution.py:20
  70.1 1.3 collective-permute-start.7
  71.4 1.7 collective-permute-done.7
  73.3 4.2 %collective-permute-start.8 = (bf16[1,3,128]{2,0,1:T(2,128)(2,1)S(1)}, bf16[1,3,128]{2,0,1:T(2,128)(2,1)S(1)}, u32[]{:S(2)}, u32[]{:S(2)}) collective-permute-start(bf16[1,3,128]{2,0,1:T(2,128)(2,1)S(1)} %get-tuple-element.19), channel_id=1, source_target_pairs={{0,1},{1,2},{2,3},{3,4},{4,5},{5,6},{6,7},{7,8},{8,9},{9,10},{10,1... | collective-permute-start | bytes 2312 | tf_op jit(solution)/shard_map/ppermute | solution.py:20
  77.5 1.5 collective-permute-start.9
  78.9 9.5 %fusion.11 = f32[64,64]{0,1:T(8,128)S(1)} fusion(f32[64,32,3,128]{3,1,2,0:T(8,128)} %param.22), kind=kOutput, calls=%fused_computation.18 | convolution fusion | flops 603979776 | bytes 3162112 | tf_op jit(solution)/shard_map/dot_general | solution.py:111
  88.5 4.8 %copy.44 = f32[64,32,3,128]{3,2,1,0:T(4,128)} copy(f32[64,32,3,128]{3,1,2,0:T(8,128)S(1)} %copy-done.2) | data formatting | bytes 6291456 | tf_op args[11]
  93.3 5.2 %reshape.115 = f32[64,12288]{1,0:T(8,128)} reshape(f32[64,32,3,128]{3,2,1,0:T(4,128)} %copy.44) | data formatting | bytes 6291456 | tf_op jit(solution)/shard_map/reshape | solution.py:120
  98.6 5.4 %dot_general.51 = f32[32,3,128,64]{2,1,0,3:T(4,128)} reshape(f32[12288,64]{0,1:T(8,128)} %bitcast.87) | data formatting | bytes 6291456 | tf_op jit(solution)/shard_map/dot_general | solution.py:119
  104.0 0.7 multiply_reduce_fusion
  104.7 6.4 %fusion.14 = f32[64]{0:T(128)S(1)} fusion(f32[64,32,3,128]{3,1,2,0:T(8,128)} %param.22, f32[32,3,128,1]{2,0,1,3:T(8,128)S(1)} %subtract_bitcast_fusion), kind=kOutput, calls=%fused_computation.19 | convolution fusion | flops 9437184 | bytes 3195136 | tf_op jit(solution)/shard_map/dot_general | solution.py:112
  111.1 45.0 %all-reduce.4 = (f32[64,64]{0,1:T(8,128)S(1)}, f32[64]{0:T(128)S(1)}, f32[]{:T(128)}) all-reduce(f32[64,64]{0,1:T(8,128)S(1)} %fusion.11, f32[64]{0:T(128)S(1)} %fusion.14, f32[]{:T(128)} %get-tuple-element.9), channel_id=1, replica_groups=mesh['fluid'=8,'solid'=4] {'fluid','solid'}, use_global_device_ids=true, to_apply=%region_2.3 | all-reduce | flops 4161 | bytes 33288 | tf_op jit(solution)/shard_map/psum | solution.py:109
  156.2 5.8 %cholesky.16 = f32[64,64]{1,0:T(8,128)S(1)} custom-call(f32[64,64]{1,0:T(8,128)S(1)} %fusion.44), custom_call_target="Cholesky" | custom-call | tf_op jit(solution)/shard_map/jit(cholesky)/cholesky | solution.py:117
  162.1 0.6 compare_reduce_fusion
  162.7 0.7 fusion.41
  163.4 4.9 %custom-call.10 = f32[1,64,64]{1,2,0:T(8,128)S(1)} custom-call(f32[1,64,64]{2,1,0:T(8,128)S(1)} %fusion.41), custom_call_target="InvertDiagBlocksLowerTriangular" | custom-call | tf_op jit(solution)/shard_map/jit(_cho_solve)/triangular_solve | solution.py:118
  168.6 5.4 %fusion.5 = f32[1,32,3,128]{3,0,2,1:T(1,128)S(1)} fusion(f32[64,1,1,1]{0,1,3,2:T(1,128)S(1)} %convolution_bitcast_fusion.1, f32[32,3,128,64]{2,1,0,3:T(4,128)} %dot_general.51), kind=kOutput, calls=%fused_computation.10 | convolution fusion | flops 9437184 | bytes 3195136 | tf_op jit(solution)/shard_map/dot_general | solution.py:119
  174.0 0.6 convert_bitcast_fusion
  174.7 0.3 convolution_convert_fusion
  174.9 0.7 all_to_all.24
  175.6 5.0 %all-to-all-start.2 = ((bf16[8,12,384]{2,1,0:T(8,128)(2,1)}), bf16[8,12,384]{2,1,0:T(8,128)(2,1)S(1)}, u32[]{:S(2)}, u32[]{:S(2)}) async-start(bf16[8,12,384]{2,1,0:T(8,128)(2,1)} %all_to_all.24), calls=%async_computation.2 | async-start | bytes 196608 | tf_op jit(solution)/shard_map/all_to_all | solution.py:129
  181.3 6.4 %all-to-all-done.2 = bf16[8,12,384]{2,1,0:T(8,128)(2,1)S(1)} async-done(((bf16[8,12,384]{2,1,0:T(8,128)(2,1)}), bf16[8,12,384]{2,1,0:T(8,128)(2,1)S(1)}, u32[]{:S(2)}, u32[]{:S(2)}) %all-to-all-start.2) | async-done | bytes 73760 | tf_op jit(solution)/shard_map/all_to_all | solution.py:129
  187.7 0.2 convolution_convert_fusion.1
  188.0 1.8 convolution_bitcast_fusion
  (46 shorter events, 1.1 us)
Async XLA Ops:
  0.6 41.3 %copy-start = (bf16[64,128,128]{2,1,0:T(8,128)(2,1)S(1)}, bf16[64,128,128]{2,1,0:T(8,128)(2,1)}, u32[]{:S(2)}) copy-start(bf16[64,128,128]{2,1,0:T(8,128)(2,1)} %param.17) | copy-start | bytes 6291460
  3.8 39.8 %all-to-all-start = ((s32[8,12,1]{1,2,0:T(1,128)}), s32[8,12,1]{1,2,0:T(1,128)S(1)}, u32[]{:S(2)}, u32[]{:S(2)}) async-start(s32[8,12,1]{1,2,0:T(1,128)} %bitcast.3), calls=%async_computation | async-start | bytes 8192 | tf_op jit(solution)/shard_map/all_to_all | solution.py:87
  11.8 9.5 %collective-permute-start = (bf16[3,1,128]{2,1,0:T(2,128)(2,1)S(1)}, bf16[3,1,128]{2,1,0:T(2,128)(2,1)S(1)}, u32[]{:S(2)}, u32[]{:S(2)}) collective-permute-start(bf16[3,1,128]{2,1,0:T(2,128)(2,1)S(1)} %get-tuple-element.17), channel_id=1, source_target_pairs={{1,0},{2,1},{3,2},{4,3},{5,4},{6,5},{7,6},{8,7},{9,8},{10,9},{11,1... | collective-permute-start | bytes 2312 | tf_op jit(solution)/shard_map/ppermute | solution.py:22
  13.1 8.2 %collective-permute-start.1 = (bf16[3,1,128]{2,1,0:T(2,128)(2,1)S(1)}, bf16[3,1,128]{2,1,0:T(2,128)(2,1)S(1)}, u32[]{:S(2)}, u32[]{:S(2)}) collective-permute-start(bf16[3,1,128]{2,1,0:T(2,128)(2,1)S(1)} %get-tuple-element.18), channel_id=1, source_target_pairs={{0,1},{1,2},{2,3},{3,4},{4,5},{5,6},{6,7},{7,8},{8,9},{9,10},{10,1... | collective-permute-start | bytes 2312 | tf_op jit(solution)/shard_map/ppermute | solution.py:20
  16.9 36.9 %collective-permute-start.2 = (bf16[1,3,128]{2,0,1:T(2,128)(2,1)S(1)}, bf16[1,3,128]{2,0,1:T(2,128)(2,1)S(1)}, u32[]{:S(2)}, u32[]{:S(2)}) collective-permute-start(bf16[1,3,128]{2,0,1:T(2,128)(2,1)S(1)} %get-tuple-element.25), channel_id=1, source_target_pairs={{0,1},{1,2},{2,3},{3,4},{4,5},{5,6},{6,7},{7,8},{8,9},{9,10},{10,1... | collective-permute-start | bytes 2312 | tf_op jit(solution)/shard_map/ppermute | solution.py:20
  20.0 33.8 %collective-permute-start.3 = (bf16[1,3,128]{2,0,1:T(2,128)(2,1)S(1)}, bf16[1,3,128]{2,0,1:T(2,128)(2,1)S(1)}, u32[]{:S(2)}, u32[]{:S(2)}) collective-permute-start(bf16[1,3,128]{2,0,1:T(2,128)(2,1)S(1)} %get-tuple-element.26), channel_id=1, source_target_pairs={{1,0},{2,1},{3,2},{4,3},{5,4},{6,5},{7,6},{8,7},{9,8},{10,9},{11,1... | collective-permute-start | bytes 2312 | tf_op jit(solution)/shard_map/ppermute | solution.py:22
  21.3 18.9 %copy-start.5 = (bf16[128]{0:T(256)(128)(2,1)S(1)}, bf16[128]{0:T(256)(128)(2,1)}, u32[]{:S(2)}) copy-start(bf16[128]{0:T(256)(128)(2,1)} %param.16) | copy-start | bytes 772
  37.5 2.7 %copy-start.1 = (bf16[3,8192,128]{2,1,0:T(8,128)(2,1)}, bf16[3,8192,128]{2,1,0:T(8,128)(2,1)S(1)}, u32[]{:S(2)}) copy-start(bf16[3,8192,128]{2,1,0:T(8,128)(2,1)S(1)} %fusion.2) | copy-start | bytes 18874372
  37.5 15.1 %copy-start.4 = (f32[32,128]{1,0:T(8,128)S(1)}, f32[32,128]{1,0:T(8,128)}, u32[]{:S(2)}) copy-start(f32[32,128]{1,0:T(8,128)} %param.21) | copy-start | bytes 49156
  37.5 22.8 %copy-start.3 = (f32[32,3,128]{2,0,1:T(8,128)S(1)}, f32[32,3,128]{2,0,1:T(8,128)}, u32[]{:S(2)}) copy-start(f32[32,3,128]{2,0,1:T(8,128)} %param.20) | copy-start | bytes 147460
  43.6 16.7 %all-to-all-start.1 = ((f32[8,12,384]{2,1,0:T(8,128)}), f32[8,12,384]{2,1,0:T(8,128)S(1)}, u32[]{:S(2)}, u32[]{:S(2)}) async-start(f32[8,12,384]{2,1,0:T(8,128)} %fusion.22), calls=%async_computation.1 | async-start | bytes 393216 | tf_op jit(solution)/shard_map/all_to_all | solution.py:86
  60.4 28.1 %copy-start.2 = (f32[64,32,3,128]{3,1,2,0:T(8,128)S(1)}, f32[64,32,3,128]{3,1,2,0:T(8,128)}, u32[]{:S(2)}) copy-start(f32[64,32,3,128]{3,1,2,0:T(8,128)} %param.23) | copy-start | bytes 9437188
  60.6 2.7 %collective-permute-start.4 = (bf16[1,3,128]{2,0,1:T(2,128)(2,1)S(1)}, bf16[1,3,128]{2,0,1:T(2,128)(2,1)S(1)}, u32[]{:S(2)}, u32[]{:S(2)}) collective-permute-start(bf16[1,3,128]{2,0,1:T(2,128)(2,1)S(1)} %get-tuple-element.23), channel_id=1, source_target_pairs={{0,1},{1,2},{2,3},{3,4},{4,5},{5,6},{6,7},{7,8},{8,9},{9,10},{10,1... | collective-permute-start | bytes 2312 | tf_op jit(solution)/shard_map/ppermute | solution.py:20
  62.0 3.6 %collective-permute-start.5 = (bf16[1,3,128]{2,0,1:T(2,128)(2,1)S(1)}, bf16[1,3,128]{2,0,1:T(2,128)(2,1)S(1)}, u32[]{:S(2)}, u32[]{:S(2)}) collective-permute-start(bf16[1,3,128]{2,0,1:T(2,128)(2,1)S(1)} %get-tuple-element.24), channel_id=1, source_target_pairs={{1,0},{2,1},{3,2},{4,3},{5,4},{6,5},{7,6},{8,7},{9,8},{10,9},{11,1... | collective-permute-start | bytes 2312 | tf_op jit(solution)/shard_map/ppermute | solution.py:22
  65.8 5.6 %collective-permute-start.6 = (bf16[1,3,128]{2,0,1:T(2,128)(2,1)S(1)}, bf16[1,3,128]{2,0,1:T(2,128)(2,1)S(1)}, u32[]{:S(2)}, u32[]{:S(2)}) collective-permute-start(bf16[1,3,128]{2,0,1:T(2,128)(2,1)S(1)} %get-tuple-element.21), channel_id=1, source_target_pairs={{0,1},{1,2},{2,3},{3,4},{4,5},{5,6},{6,7},{7,8},{8,9},{9,10},{10,1... | collective-permute-start | bytes 2312 | tf_op jit(solution)/shard_map/ppermute | solution.py:20
  70.1 3.1 %collective-permute-start.7 = (bf16[1,3,128]{2,0,1:T(2,128)(2,1)S(1)}, bf16[1,3,128]{2,0,1:T(2,128)(2,1)S(1)}, u32[]{:S(2)}, u32[]{:S(2)}) collective-permute-start(bf16[1,3,128]{2,0,1:T(2,128)(2,1)S(1)} %get-tuple-element.22), channel_id=1, source_target_pairs={{1,0},{2,1},{3,2},{4,3},{5,4},{6,5},{7,6},{8,7},{9,8},{10,9},{11,1... | collective-permute-start | bytes 2312 | tf_op jit(solution)/shard_map/ppermute | solution.py:22
  73.3 30.7 %collective-permute-start.8 = (bf16[1,3,128]{2,0,1:T(2,128)(2,1)S(1)}, bf16[1,3,128]{2,0,1:T(2,128)(2,1)S(1)}, u32[]{:S(2)}, u32[]{:S(2)}) collective-permute-start(bf16[1,3,128]{2,0,1:T(2,128)(2,1)S(1)} %get-tuple-element.19), channel_id=1, source_target_pairs={{0,1},{1,2},{2,3},{3,4},{4,5},{5,6},{6,7},{7,8},{8,9},{9,10},{10,1... | collective-permute-start | bytes 2312 | tf_op jit(solution)/shard_map/ppermute | solution.py:20
  77.5 26.5 %collective-permute-start.9 = (bf16[1,3,128]{2,0,1:T(2,128)(2,1)S(1)}, bf16[1,3,128]{2,0,1:T(2,128)(2,1)S(1)}, u32[]{:S(2)}, u32[]{:S(2)}) collective-permute-start(bf16[1,3,128]{2,0,1:T(2,128)(2,1)S(1)} %get-tuple-element.20), channel_id=1, source_target_pairs={{1,0},{2,1},{3,2},{4,3},{5,4},{6,5},{7,6},{8,7},{9,8},{10,9},{11,1... | collective-permute-start | bytes 2312 | tf_op jit(solution)/shard_map/ppermute | solution.py:22
  175.6 12.1 %all-to-all-start.2 = ((bf16[8,12,384]{2,1,0:T(8,128)(2,1)}), bf16[8,12,384]{2,1,0:T(8,128)(2,1)S(1)}, u32[]{:S(2)}, u32[]{:S(2)}) async-start(bf16[8,12,384]{2,1,0:T(8,128)(2,1)} %all_to_all.24), calls=%async_computation.2 | async-start | bytes 196608 | tf_op jit(solution)/shard_map/all_to_all | solution.py:129
where the time goes:
time: 192 us; the launch traced here: 191 us
  blocking collectives  45 us (23%)
  starting transfers between devices  43.7 us (23%)
  matrix products  43.7 us (23%)
  local copies, waits for them, and re-layouts  21.1 us (11%)
  other arithmetic  17.6 us (9%)
  waiting for transfers between devices  17 us (9%)
  between operations  2.85 us (1%)
    psum x1, blocking collectives, per_device(): lax.psum((jnp.dot(flat_res, flat_res.T, precision=lax.Precision.HIGHEST),...  45 us
    dot_general x1, matrix products, per_device(): jnp.dot(flow.reshape(-1, normal), normal_operator, preferred_element_type...  16.1 us
    ppermute x5, starting transfers between devices, with_halo(): lax.ppermute(tail, axis, [(i, (i + 1) % count) for i in range(ends)])  15.9 us
    dot_general x1, matrix products, per_device(): jnp.dot(flat_res, flat_res.T, precision=lax.Precision.HIGHEST)  9.55 us
    all_to_all x1, starting transfers between devices, per_device(): lax.all_to_all(outgoing, 'fluid', split_axis=0, concat_axis=0, tiled=True)  8.92 us
    unnamed x13, local copies, waits for them, and re-layouts  7.55 us
    all_to_all x1, starting transfers between devices, per_device(): lax.all_to_all(labels, 'fluid', split_axis=0, concat_axis=0, tiled=True)  7.28 us
    ppermute x5, starting transfers between devices, with_halo(): lax.ppermute(head, axis, [((i + 1) % count, i) for i in range(ends)])  6.63 us
  transfers between devices with their start and end apart: 13, of which 4 were waited for; matrix products, arithmetic and copies ran while one was open for 25% of the time, Pallas kernels for 0%

commit v1 on v0

v1 whole, which is shorter than its diff:
```python
import jax
import jax.numpy as jnp
from jax import lax
from jax.experimental import pallas as pl
from jax.experimental.pallas import tpu as pltpu
from jax.sharding import PartitionSpec as P

SWEEPS = 4
AXES = ("fluid", "solid")
LANES = 128
spread_rate = 0.25
f32 = jnp.float32
bf16 = jnp.bfloat16
HIGHEST = lax.Precision.HIGHEST
VMEM = pltpu.MemorySpace.VMEM
SMEM = pltpu.MemorySpace.SMEM
ANY = pl.ANY


def up_to(value, step):
    return -(-value // step) * step


def dot(a, b, precision=None):
    return lax.dot_general(a, b, (((1,), (0,)), ((), ())), precision=precision, preferred_element_type=f32)


def dot_nt(a, b, precision=None):
    return lax.dot_general(a, b, (((1,), (1,)), ((), ())), precision=precision, preferred_element_type=f32)


def dot_tn(a, b, precision=None):
    return lax.dot_general(a, b, (((0,), (0,)), ((), ())), precision=precision, preferred_element_type=f32)


def iota(shape, dim):
    return lax.broadcasted_iota(jnp.int32, shape, dim)


def split3(value):
    high = value.astype(bf16)
    rest = value - high.astype(f32)
    middle = rest.astype(bf16)
    low = (rest - middle.astype(f32)).astype(bf16)
    return high, middle, low


def spec(memory):
    return pl.BlockSpec(memory_space=memory)


def largest_divisor(value, most):
    return max(d for d in range(1, most + 1) if value % d == 0)


def first_stage(me, owner, local_row, history, head, tail, devices, groups, inner, slots, capacity):
    count, lines, _ = history.shape
    comps = head.shape[0]
    blocks = owner.shape[1]
    part = count // groups
    half = part // 2
    chunk = largest_divisor(lines, 16)

    def kernel(me_ref, owner_ref, row_ref, hist_ref, head_ref, tail_ref, send_ref, chosen_ref, label_ref, turned, acc, sems):
        for k in range(lines):
            pltpu.make_async_copy(hist_ref.at[:, k, :], turned.at[k], sems.at[k]).start()
        send_ref[...] = jnp.zeros(send_ref.shape, f32)
        owners = owner_ref[...]
        names = jnp.where(owners == iota((groups, blocks), 0), 1.0, 0.0)
        before = jnp.where(iota((blocks, blocks), 0) < iota((blocks, blocks), 1), 1.0, 0.0)
        earlier = dot(names.astype(bf16), before.astype(bf16))
        numbers = (row_ref[...] + 1).astype(f32)
        place = iota((slots, blocks), 0).astype(f32)
        for g in range(groups):
            mine = jnp.where((earlier[g : g + 1] == place) & (names[g : g + 1] > 0.5), 1.0, 0.0)
            chosen_ref[g * slots : (g + 1) * slots, :] = mine.astype(bf16)
        labels = dot_nt(jnp.broadcast_to(numbers, (8, blocks)).astype(bf16), chosen_ref[...])
        for g in range(groups):
            label_ref[g : g + 1, :] = jnp.concatenate(
                [labels[0:1, g * slots : (g + 1) * slots], jnp.zeros((1, LANES - slots), f32)], axis=1
            )
        acc[...] = jnp.zeros(acc.shape, f32)

        def body(step, carry):
            pieces = []
            for k in range(chunk):
                line = step * chunk + k
                pltpu.make_async_copy(hist_ref.at[:, line, :], turned.at[line], sems.at[line]).wait()
                pieces.append(turned[line])
            parts = split3(jnp.concatenate(pieces, axis=1))
            left = jnp.concatenate(parts, axis=0)
            right = jnp.concatenate(parts + (jnp.zeros_like(parts[0]),), axis=0)
            acc[...] += dot_nt(left, right)
            return carry

        lax.fori_loop(0, lines // chunk, body, 0)
        total = acc[0:count, :] + acc[count : 2 * count, :] + acc[2 * count :, :]
        wide = total[:, :LANES] + total[:, LANES:]
        wide = wide + pltpu.roll(wide, LANES // 2, 1)
        low_lane = iota((half, LANES), 1) < LANES // 2
        for g in range(groups):
            packed = jnp.where(
                low_lane, wide[g * part : g * part + half], wide[g * part + half : (g + 1) * part]
            )
            for s in range(inner):
                send_ref[g * inner + s, 0:half, :] = packed
        own = me_ref[0]

        @pl.when(own > 0)
        def _():
            rows = head_ref[...].astype(f32)
            for c in range(comps):
                send_ref[own - 1, 4 + c : 5 + c, :] = rows[c, 0:1, :]

        @pl.when(own < devices - 1)
        def _():
            rows = tail_ref[...].astype(f32)
            for c in range(comps):
                send_ref[own + 1, 4 + c : 5 + c, :] = rows[c, 15:16, :]

    return pl.pallas_call(
        kernel,
        out_shape=(
            jax.ShapeDtypeStruct((devices, 8, LANES), f32),
            jax.ShapeDtypeStruct((groups * slots, blocks), bf16),
            jax.ShapeDtypeStruct((groups, LANES), f32),
        ),
        in_specs=[spec(SMEM), spec(VMEM), spec(VMEM), spec(ANY), spec(VMEM), spec(VMEM)],
        out_specs=(spec(VMEM), spec(VMEM), spec(VMEM)),
        scratch_shapes=[
            pltpu.VMEM((lines, count, LANES), f32),
            pltpu.VMEM((3 * count, 4 * count), f32),
            pltpu.SemaphoreType.DMA((lines,)),
        ],
        name="gram",
    )(me, owner, local_row, history, head, tail)


def flow_stage(flow, wall_motion, normal_operator, coupling, stencil, rbf, tile):
    comps, points, normal = flow.shape
    steps = points // tile
    inside = tile // LANES

    def kernel(flow_ref, prev_ref, next_ref, motion_ref, op_ref, coup_ref, sten_ref, rbf_ref, new_ref, map_ref, pre_ref, tr_ref, edge_ref, quarter, cols):
        i = pl.program_id(0)
        for c in range(comps):
            for j in range(inside):
                cols[c * inside + j : c * inside + j + 1, :] = motion_ref[c : c + 1, j * LANES : (j + 1) * LANES]
        turned = jnp.transpose(cols[...])
        coup = coup_ref[...]
        op = op_ref[...]
        sten = jnp.broadcast_to(sten_ref[...], (8, normal))
        row8 = iota((8, tile), 0)
        keep_prev = jnp.where(i > 0, spread_rate, 0.0)
        keep_next = jnp.where(i < steps - 1, spread_rate, 0.0)
        trac = None
        for c in range(comps):
            quarter[0:8, :] = prev_ref[c, 8:16, :].astype(f32) * keep_prev
            quarter[8 : 8 + tile, :] = flow_ref[c].astype(f32) * spread_rate
            quarter[8 + tile : 16 + tile, :] = next_ref[c, 0:8, :].astype(f32) * keep_next
            for j in range(inside):
                o = j * LANES
                drift = dot(flow_ref[c, o : o + LANES, :], op)
                mid = quarter[8 + o : 8 + o + LANES, :]
                around = quarter[7 + o : 7 + o + LANES, :] + quarter[9 + o : 9 + o + LANES, :]
                k = c * inside + j
                fresh = drift + (mid + mid) + around + turned[:, k : k + 1] * coup
                new_ref[c, o : o + LANES, :] = fresh.astype(bf16)
                if j == 0:

                    @pl.when(i == 0)
                    def _():
                        pre_ref[0, 4 + c : 5 + c, :] = fresh[0:1, :]
                        edge_ref[0, c] = fresh[0:16, :].astype(bf16)

                if j == inside - 1:

                    @pl.when(i == steps - 1)
                    def _():
                        pre_ref[1, 4 + c : 5 + c, :] = fresh[LANES - 1 : LANES, :]
                        edge_ref[1, c] = fresh[LANES - 16 : LANES, :].astype(bf16)

            row = dot_nt(sten, new_ref[c])
            trac = row if trac is None else jnp.where((row8 == c) | (row8 == 4 + c), row, trac)
        trac = trac.astype(bf16)

        @pl.when(i == 0)
        def _():
            tr_ref[0] = trac[:, 0:LANES].astype(f32)

        @pl.when(i == steps - 1)
        def _():
            tr_ref[1] = trac[:, tile - LANES : tile].astype(f32)

        for j in range(inside):
            got = dot(trac[:, j * LANES : (j + 1) * LANES], rbf_ref[j])
            for c in range(comps):
                map_ref[c, j : j + 1, :] = got[4 + c : 5 + c, :]

    per = tile // 16
    last = points // 16 - 1
    fixed2 = lambda i: (0, 0)
    return pl.pallas_call(
        kernel,
        grid=(steps,),
        out_shape=(
            jax.ShapeDtypeStruct(flow.shape, bf16),
            jax.ShapeDtypeStruct((comps, points // LANES, LANES), f32),
            jax.ShapeDtypeStruct((2, 8, LANES), f32),
            jax.ShapeDtypeStruct((2, 8, LANES), f32),
            jax.ShapeDtypeStruct((2, comps, 16, LANES), bf16),
        ),
        in_specs=[
            pl.BlockSpec((comps, tile, normal), lambda i: (0, i, 0)),
            pl.BlockSpec((comps, 16, normal), lambda i: (0, jnp.maximum(i * per - 1, 0), 0)),
            pl.BlockSpec((comps, 16, normal), lambda i: (0, jnp.minimum((i + 1) * per, last), 0)),
            pl.BlockSpec((comps, tile), lambda i: (0, i)),
            pl.BlockSpec((normal, normal), fixed2),
            pl.BlockSpec((1, normal), fixed2),
            pl.BlockSpec((1, normal), fixed2),
            pl.BlockSpec((inside, LANES, LANES), lambda i: (i, 0, 0)),
        ],
        out_specs=(
            pl.BlockSpec((comps, tile, normal), lambda i: (0, i, 0)),
            pl.BlockSpec((comps, inside, LANES), lambda i: (0, i, 0)),
            pl.BlockSpec((2, 8, LANES), lambda i: (0, 0, 0)),
            pl.BlockSpec((2, 8, LANES), lambda i: (0, 0, 0)),
            pl.BlockSpec((2, comps, 16, LANES), lambda i: (0, 0, 0, 0)),
        ),
        scratch_shapes=[pltpu.VMEM((tile + 16, LANES), f32), pltpu.VMEM((LANES, LANES), f32)],
        name="flow",
    )(flow, flow, flow, wall_motion, normal_operator, coupling, stencil, rbf)


def pack_stage(me, got, pre, tr, edge, stencil, rbf, mapped, chosen, labels, new_flow, devices, groups, slots, capacity, count, width):
    comps, blocks, _ = mapped.shape
    points = new_flow.shape[1]
    part = count // groups
    half = part // 2

    def kernel(me_ref, got_ref, pre_ref, tr_ref, edge_ref, sten_ref, rbf_first, rbf_last, map_ref, chosen_ref, label_ref, flow_in, flow_out, send_ref, tiles, sems):
        own = me_ref[0]
        sten = sten_ref[...].astype(f32)
        lane = iota((8, LANES), 1)
        row16 = iota((16, LANES), 0)
        fixed = []
        for e in range(2):
            if e == 0:
                halo = got_ref[jnp.maximum(own - 1, 0)] * jnp.where(own > 0, spread_rate, 0.0)
            else:
                halo = got_ref[jnp.minimum(own + 1, devices - 1)] * jnp.where(own < devices - 1, spread_rate, 0.0)
            fresh = (pre_ref[e] + halo).astype(bf16).astype(f32)
            at = 0 if e == 0 else 15
            for c in range(comps):
                tiles[e, c] = jnp.where(row16 == at, fresh[4 + c : 5 + c, :], edge_ref[e, c].astype(f32)).astype(bf16)
            start = 0 if e == 0 else points - 16
            pltpu.make_async_copy(tiles.at[e], flow_out.at[:, pl.ds(start, 16), :], sems.at[e]).start()
            point = jnp.sum(fresh * sten, axis=1, keepdims=True)
            trac = jnp.where(lane == (0 if e == 0 else LANES - 1), point, tr_ref[e]).astype(bf16)
            fixed.append(dot(trac, (rbf_first if e == 0 else rbf_last)[0]))
        total = got_ref[0]
        for d in range(1, devices):
            total = total + got_ref[d]
        swapped = pltpu.roll(pltpu.roll(total, LANES // 2, 1), half, 0)
        rows = iota((8, LANES), 0)
        gram = jnp.where(rows < half, total, swapped)
        gram = jnp.where(rows < part, gram, 0.0)
        pieces = split3(gram)
        block = iota((blocks, LANES), 0)
        label_row = iota((slots, LANES), 0) == capacity
        for c in range(comps):
            here = jnp.where(block == 0, fixed[0][4 + c : 5 + c, :], map_ref[c])
            here = jnp.where(block == blocks - 1, fixed[1][4 + c : 5 + c, :], here)
            out = dot(chosen_ref[...], here.astype(bf16))
            for g in range(groups):
                cut = out[g * slots : (g + 1) * slots, :]
                if c == 0:
                    cut = jnp.where(label_row, label_ref[g : g + 1, :], cut)
                send_ref[g, 0:slots, c * LANES : (c + 1) * LANES] = cut.astype(bf16)
                send_ref[g, slots : slots + 8, c * LANES : (c + 1) * LANES] = pieces[c]
        for e in range(2):
            start = 0 if e == 0 else points - 16
            pltpu.make_async_copy(tiles.at[e], flow_out.at[:, pl.ds(start, 16), :], sems.at[e]).wait()

    full = lambda a: pl.BlockSpec(a.shape, lambda i: (0,) * a.ndim)
    return pl.pallas_call(
        kernel,
        grid=(1,),
        out_shape=(
            jax.ShapeDtypeStruct(new_flow.shape, bf16),
            jax.ShapeDtypeStruct((groups, slots + 8, comps * width), bf16),
        ),
        in_specs=[
            spec(SMEM), full(got), full(pre), full(tr), full(edge), full(stencil),
            pl.BlockSpec((1, LANES, LANES), lambda i: (0, 0, 0)),
            pl.BlockSpec((1, LANES, LANES), lambda i: (blocks - 1, 0, 0)),
            full(mapped), full(chosen), full(labels), spec(ANY),
        ],
        out_specs=(spec(ANY), pl.BlockSpec((groups, slots + 8, comps * width), lambda i: (0, 0, 0))),
        scratch_shapes=[pltpu.VMEM((2, comps, 16, LANES), bf16), pltpu.SemaphoreType.DMA((2,))],
        input_output_aliases={11: 0},
        name="pack",
    )(me, got, pre, tr, edge, stencil, rbf, rbf, mapped, chosen, labels, new_flow)


def place_stage(arrived, displacement, stiffness, groups, slots, capacity, count):
    comps, rows, width = displacement.shape
    part = count // groups
    depth = SWEEPS
    short = depth - 1

    def kernel(got_ref, disp_ref, stiff_ref, force_ref, gram_ref, label_ref, head_ref, tail_ref):
        index = iota((rows, slots), 0).astype(f32) + 1.0
        total = jnp.zeros((rows, comps * width), f32)
        for g in range(groups):
            labels = got_ref[g, capacity : capacity + 1, 0:LANES].astype(f32)
            label_ref[g : g + 1, :] = labels
            placed = jnp.where(labels[:, 0:slots] == index, 1.0, 0.0).astype(bf16)
            total = total + dot(placed, got_ref[g, 0:slots, :])
            extra = got_ref[g, slots : slots + 8, :].astype(f32)
            value = extra[:, 0:LANES] + extra[:, LANES : 2 * LANES] + extra[:, 2 * LANES : 3 * LANES]
            gram_ref[g * part : (g + 1) * part, :] = value[0:part, 0:count]
        for c in range(comps):
            force_ref[c] = total[:, c * width : (c + 1) * width]
        for c in range(comps):
            head_ref[c * short : (c + 1) * short, :] = force_ref[c, 0:short, :]
            tail_ref[c * short : (c + 1) * short, :] = force_ref[c, rows - short : rows, :]
            at = comps * short + c * depth
            head_ref[at : at + depth, :] = disp_ref[c, 0:depth, :]
            tail_ref[at : at + depth, :] = disp_ref[c, rows - depth : rows, :]
        at = comps * (short + depth)
        head_ref[at : at + short, :] = stiff_ref[0:short, :]
        tail_ref[at : at + short, :] = stiff_ref[rows - short : rows, :]

    edge = (comps * (short + depth) + short, width)
    return pl.pallas_call(
        kernel,
        out_shape=(
            jax.ShapeDtypeStruct((comps, rows, width), f32),
            jax.ShapeDtypeStruct((count, count), f32),
            jax.ShapeDtypeStruct((groups, LANES), f32),
            jax.ShapeDtypeStruct(edge, f32),
            jax.ShapeDtypeStruct(edge, f32),
        ),
        name="place",
    )(arrived, displacement, stiffness)


def sweep_stage(me, force, displacement, stiffness, before, after, history, devices):
    comps, rows, width = displacement.shape
    count, lines, _ = history.shape
    depth = SWEEPS
    short = depth - 1
    rim = 8
    whole = rows + 2 * rim

    def kernel(me_ref, force_ref, disp_ref, stiff_ref, before_ref, after_ref, hist_ref, solved_ref, send_ref, ext, sums):
        own = me_ref[0]
        row = iota((whole, width), 0)
        lane = iota((whole, width), 1)
        lowest = jnp.where(own > 0, rim - depth, rim)
        highest = jnp.where(own < devices - 1, rim + rows + depth, rim + rows)
        valid = jnp.where((row >= lowest) & (row < highest), 1.0, 0.0)
        at = comps * (short + depth)
        ext[...] = jnp.zeros(ext.shape, f32)
        ext[0, rim - short : rim, :] = before_ref[at : at + short, :]
        ext[0, rim : rim + rows, :] = stiff_ref[...]
        ext[0, rim + rows : rim + rows + short, :] = after_ref[at : at + short, :]
        scale = valid / (4.0 + ext[0])
        left_ok = jnp.where(lane > 0, 1.0, 0.0)
        right_ok = jnp.where(lane < width - 1, 1.0, 0.0)
        squares = jnp.zeros((8, width), f32)
        residuals = []
        for c in range(comps):
            f = 1 + 2 * c
            ext[f, rim - short : rim, :] = before_ref[c * short : (c + 1) * short, :]
            ext[f, rim : rim + rows, :] = force_ref[c]
            ext[f, rim + rows : rim + rows + short, :] = after_ref[c * short : (c + 1) * short, :]
            d = comps * short + c * depth
            ext[f + 1, rim - depth : rim, :] = before_ref[d : d + depth, :]
            ext[f + 1, rim : rim + rows, :] = disp_ref[c]
            ext[f + 1, rim + rows : rim + rows + depth, :] = after_ref[d : d + depth, :]
        for c in range(comps):
            push = ext[1 + 2 * c]
            solved = ext[2 + 2 * c]
            for sweep in range(SWEEPS):
                beside = pltpu.roll(solved, 1, 0) + pltpu.roll(solved, whole - 1, 0)
                beside = beside + pltpu.roll(solved, 1, 1) * left_ok + pltpu.roll(solved, width - 1, 1) * right_ok
                solved = (push + beside) * scale
            mine = solved[rim : rim + rows, :]
            solved_ref[c] = mine
            residual = mine - disp_ref[c]
            residuals.append(residual)
            square = residual * residual
            for k in range(rows // 8):
                squares = squares + square[8 * k : 8 * k + 8, :]
        sums[count:, :] = jnp.zeros((LANES - count, width), f32)
        sums[count : count + 1, :] = jnp.sum(squares, axis=0, keepdims=True)
        flat = jnp.concatenate(residuals, axis=0)
        for j in range(count):
            prod = hist_ref[j] * flat
            sums[j : j + 1, :] = jnp.sum(prod, axis=0, keepdims=True)
        line = dot_nt(jnp.ones((8, width), f32), sums[...], HIGHEST)
        for d in range(devices):
            send_ref[d] = line[0:1, :]

    return pl.pallas_call(
        kernel,
        out_shape=(
            jax.ShapeDtypeStruct((comps, rows, width), f32),
            jax.ShapeDtypeStruct((devices, 1, LANES), f32),
        ),
        in_specs=[spec(SMEM)] + [spec(VMEM)] * 6,
        out_specs=(spec(VMEM), spec(VMEM)),
        scratch_shapes=[pltpu.VMEM((1 + 2 * comps, whole, width), f32), pltpu.VMEM((LANES, width), f32)],
        name="sweeps",
    )(me, force, displacement, stiffness, before, after, history)


def update_stage(arrived, inverse, inverse_t, history, solved, labels, groups, slots):
    comps, rows, width = solved.shape
    count, lines, _ = history.shape

    def kernel(got_ref, inv_ref, invt_ref, hist_ref, solved_ref, label_ref, next_ref, reply_ref, line_ref, coeff):
        line = jnp.sum(got_ref[...], axis=0)
        line_ref[...] = line
        half = jnp.sum(inv_ref[...] * line[:, 0:count], axis=1, keepdims=True)
        coeff[...] = -dot(invt_ref[...], jnp.broadcast_to(half, (count, width)), HIGHEST)

        def body(j, total):
            return total + hist_ref[j] * coeff[pl.ds(j, 1), :]

        update = lax.fori_loop(0, count, body, jnp.zeros((lines, width), f32), unroll=8)
        shell = []
        for c in range(comps):
            fresh = solved_ref[c] + update[c * rows : (c + 1) * rows, :]
            next_ref[c] = fresh
            shell.append(fresh.astype(bf16))
        shell = jnp.concatenate(shell, axis=1)
        index = iota((rows, slots), 0).astype(f32) + 1.0
        for g in range(groups):
            placed = jnp.where(label_ref[g : g + 1, 0:slots] == index, 1.0, 0.0).astype(bf16)
            reply_ref[g] = dot_tn(placed, shell).astype(bf16)

    return pl.pallas_call(
        kernel,
        out_shape=(
            jax.ShapeDtypeStruct((comps, rows, width), f32),
            jax.ShapeDtypeStruct((groups, slots, comps * width), bf16),
            jax.ShapeDtypeStruct((1, LANES), f32),
        ),
        scratch_shapes=[pltpu.VMEM((count, width), f32)],
        name="update",
    )(arrived, inverse, inverse_t, history, solved, labels)


def wall_stage(returned, chosen, rbf, comps):
    blocks, block, width = rbf.shape
    groups, slots, _ = returned.shape

    def kernel(got_ref, chosen_ref, rbf_ref, out_ref, shells):
        got = jnp.concatenate([got_ref[g] for g in range(groups)], axis=0)
        fetched = dot_tn(chosen_ref[...], got)
        shells[...] = jnp.zeros(shells.shape, f32)
        for c in range(comps):
            shells[:, c, :] = fetched[:, c * width : (c + 1) * width]
        for b in range(blocks):
            res = dot_nt(shells[b].astype(bf16), rbf_ref[b])
            out_ref[:, b * block : (b + 1) * block] = res[0:comps, :]

    return pl.pallas_call(
        kernel,
        out_shape=jax.ShapeDtypeStruct((comps, blocks * block), f32),
        scratch_shapes=[pltpu.VMEM((blocks, 8, width), f32)],
        name="wall",
    )(returned, chosen, rbf)


def per_device(
    flow,
    wall_motion,
    normal_operator,
    wall_coupling,
    wall_stencil,
    rbf_blocks,
    block_owner,
    block_row,
    displacement,
    stiffness,
    residual_history,
    solution_history,
):
    groups = lax.axis_size("fluid")
    inner = lax.axis_size("solid")
    devices = groups * inner
    comps, points, normal = flow.shape
    blocks, block, width = rbf_blocks.shape
    count = residual_history.shape[0]
    rows = displacement.shape[0]
    capacity = max(2, (3 * blocks + 2 * groups - 1) // (2 * groups))
    slots = up_to(capacity + 1, 16)
    me = lax.axis_index(AXES).astype(jnp.int32).reshape(1)

    disp = displacement.transpose(1, 0, 2)
    res_hist = residual_history.transpose(0, 2, 1, 3).reshape(count, comps * rows, width)
    sol_hist = solution_history.transpose(0, 2, 1, 3).reshape(count, comps * rows, width)
    owner = block_owner.reshape(1, blocks)
    local_row = block_row.reshape(1, blocks)
    coupling = wall_coupling.reshape(1, normal)
    stencil = wall_stencil.reshape(1, normal)

    send, chosen, labels = first_stage(
        me, owner, local_row, res_hist, flow[:, :16, :], flow[:, points - 16 :, :], devices, groups, inner, slots, capacity
    )
    got = lax.all_to_all(send, AXES, 0, 0, tiled=True)
    tile = 1024 if points % 1024 == 0 else points
    new_flow, mapped, pre, tr, edge = flow_stage(
        flow, wall_motion, normal_operator, coupling, stencil, rbf_blocks, tile
    )
    new_flow, send = pack_stage(
        me, got, pre, tr, edge, stencil, rbf_blocks, mapped, chosen, labels, new_flow,
        devices, groups, slots, capacity, count, width,
    )
    arrived = lax.all_to_all(send, "fluid", 0, 0, tiled=True)
    force, gram, placed_labels, head, tail = place_stage(arrived, disp, stiffness, groups, slots, capacity, count)
    before = lax.ppermute(tail, AXES, [(i, i + 1) for i in range(devices - 1)])
    after = lax.ppermute(head, AXES, [(i + 1, i) for i in range(devices - 1)])
    lower = jnp.linalg.cholesky(gram)
    inverse = jax.scipy.linalg.solve_triangular(lower, jnp.eye(count, dtype=f32), lower=True)
    solved, send = sweep_stage(me, force, disp, stiffness, before, after, res_hist, devices)
    got = lax.all_to_all(send, AXES, 0, 0, tiled=True)
    fresh, reply, line = update_stage(got, inverse, inverse.T, sol_hist, solved, placed_labels, groups, slots)
    returned = lax.all_to_all(reply, "fluid", 0, 0, tiled=True)
    wall_next = wall_stage(returned, chosen, rbf_blocks, comps)
    return (new_flow, fresh.transpose(1, 0, 2), wall_next, jnp.sqrt(line[0, count]))


def solution(mesh):
    return jax.shard_map(
        per_device,
        mesh=mesh,
        in_specs=(
            P(None, ("fluid", "solid"), None),
            P(None, ("fluid", "solid")),
            P(),
            P(),
            P(),
            P(("fluid", "solid"), None, None),
            P(("fluid", "solid"), None),
            P(("fluid", "solid"), None),
            P(("fluid", "solid"), None, None),
            P(("fluid", "solid"), None),
            P(None, ("fluid", "solid"), None, None),
            P(None, ("fluid", "solid"), None, None),
        ),
        out_specs=(
            P(None, ("fluid", "solid"), None),
            P(("fluid", "solid"), None, None),
            P(None, ("fluid", "solid")),
            P(),
        ),
        check_vma=False,
    )
```

time: 192 us -> 104 us (0.54)
  matrix products: 43.7 us -> 0.21 us
  Pallas kernels: 0 us -> 37.4 us
  blocking collectives: 45 us -> 13.4 us
  starting transfers between devices: 43.7 us -> 19.1 us
  local copies, waits for them, and re-layouts: 21.1 us -> 6.64 us
  waiting for transfers between devices: 17 us -> 11.3 us
  other arithmetic: 17.6 us -> 12.8 us
    psum x1 -> x0, blocking collectives: 45 us -> none  [per_device(): lax.psum((jnp.dot(flat_res, flat_res.T, precision=lax.Precision.HIGHEST),...]
    dot_general x11 -> x0, matrix products: 43.4 us -> none  [the longest x1 16.1 us: per_device(): jnp.dot(flow.reshape(-1, normal), normal_operator, preferred_element_type...]
    pallas_call x0 -> x7, Pallas kernels: none -> 37.4 us  [the longest x1 16.7 us: flow_stage(): pl.pallas_call(kernel, grid=(steps,), out_shape=(jax.ShapeDtypeStruct(flo...]
    ppermute x10 -> x2, starting transfers between devices: 22.6 us -> 2.57 us  [the longest x1 1.29 us: per_device(): after = lax.ppermute(head, AXES, [(i + 1, i) for i in range(devices - 1)])]
    all_to_all x0 -> x1, blocking collectives: none -> 13.4 us  [per_device(): arrived = lax.all_to_all(send, 'fluid', 0, 0, tiled=True)]
    dot_general x1 -> x0, local copies, waits for them, and re-layouts: 5.44 us -> none  [per_device(): jnp.dot(coeff, solution_history.reshape(history, -1), precision=lax.Preci...]
    reshape x3 -> x0, local copies, waits for them, and re-layouts: 5.29 us -> none  [the longest x1 5.21 us: per_device(): solution_history.reshape(history, -1)]
    unnamed x13 -> x12, local copies, waits for them, and re-layouts: 7.55 us -> 2.48 us
  transfers between devices with their start and end apart: 13 -> 5, of which waited for: 4 -> 2; matrix products, arithmetic and copies ran while one was open for 25% -> 15% of each run, Pallas kernels for 0% -> 16%
where the time goes in v1:
time: 104 us
  Pallas kernels  37.4 us (36%)
  starting transfers between devices  19.1 us (18%)
  blocking collectives  13.4 us (13%)
  other arithmetic  12.8 us (12%)
  waiting for transfers between devices  11.3 us (11%)
  local copies, waits for them, and re-layouts  6.64 us (6%)
  between operations  2.58 us (2%)
    pallas_call x1, Pallas kernels, flow_stage(): pl.pallas_call(kernel, grid=(steps,), out_shape=(jax.ShapeDtypeStruct(flo...  16.7 us
    all_to_all x1, blocking collectives, per_device(): arrived = lax.all_to_all(send, 'fluid', 0, 0, tiled=True)  13.4 us
    all_to_all x2, starting transfers between devices, per_device(): got = lax.all_to_all(send, AXES, 0, 0, tiled=True)  13.1 us
    another operation x3, other arithmetic, per_device(): lower = jnp.linalg.cholesky(gram)  6.52 us
    all_to_all x2, waiting for transfers between devices, per_device(): got = lax.all_to_all(send, AXES, 0, 0, tiled=True)  6.18 us
    pallas_call x1, Pallas kernels, first_stage(): pl.pallas_call(kernel, out_shape=(jax.ShapeDtypeStruct((devices, 8, LANES...  6.05 us
    another operation x2, other arithmetic, per_device(): jax.scipy.linalg.solve_triangular(lower, jnp.eye(count, dtype=f32), lower...  5.55 us
    all_to_all x1, waiting for transfers between devices, per_device(): returned = lax.all_to_all(reply, 'fluid', 0, 0, tiled=True)  5.09 us
  transfers between devices with their start and end apart: 5, of which 2 were waited for; matrix products, arithmetic and copies ran while one was open for 15% of the time, Pallas kernels for 16%

profile of v1, /device:TPU:0, one launch (start us, length us, event | category | flops | bytes accessed | tf_op | source)
XLA Modules:
  0.0 103.5 jit_solution(16034370946715794957)
XLA Ops:
  0.6 1.3 %fusion.4 = (bf16[3,16,128]{2,1,0:T(8,128)(2,1)}, bf16[3,16,128]{2,1,0:T(8,128)(2,1)}) fusion(bf16[3,8192,128]{2,1,0:T(8,128)(2,1)} %next_ref.1), kind=kLoop, calls=%fused_computation.10 | loop fusion | bytes 49152 | tf_op jit(solution)/shard_map/slice | solution.py:513
  2.0 6.1 %gram.1 = (f32[32,8,128]{2,1,0:T(8,128)}, bf16[128,64]{1,0:T(8,128)(2,1)}, f32[8,128]{1,0:T(8,128)}) custom-call(s32[1]{0:T(128)} %bitcast.me_ref, s32[1,64]{1,0:T(1,128)} %bitcast.32, s32[1,64]{1,0:T(1,128)} %bitcast.33, f32[64,96,128]{2,1,0:T(8,128)} %bitcast.24, bf16[3,16,128]{2,1,0:T(8,128)(2,1)} %get-tuple-element.45.head_ref, ...), custom_call_target="tpu_custom_call" | custom-call | tf_op jit(solution)/shard_map/gram/pallas_call | solution.py:121
  8.0 7.3 %all-to-all-start = ((f32[32,8,128]{2,1,0:T(8,128)}), f32[32,8,128]{2,1,0:T(8,128)S(1)}, u32[]{:S(2)}, u32[]{:S(2)}) async-start(f32[32,8,128]{2,1,0:T(8,128)} %get-tuple-element.24), calls=%async_computation | async-start | bytes 262144 | tf_op jit(solution)/shard_map/all_to_all | solution.py:515
  15.4 16.7 %flow.1 = (bf16[3,8192,128]{2,1,0:T(8,128)(2,1)}, f32[3,64,128]{2,1,0:T(8,128)}, f32[2,8,128]{2,1,0:T(8,128)}, f32[2,8,128]{2,1,0:T(8,128)}, bf16[2,3,16,128]{3,2,1,0:T(8,128)(2,1)}) custom-call(bf16[3,8192,128]{2,1,0:T(8,128)(2,1)} %next_ref.1, bf16[3,8192,128]{2,1,0:T(8,128)(2,1)} %next_ref.1, bf16[3,8192,128]{2,1,0:T(8,128)(2,1)} %next_ref.1, ...), custom_call_target="tpu_custom_call" | custom-call | tf_op jit(solution)/shard_map/flow/pallas_call | solution.py:203
  32.0 0.0 all-to-all-done.got_ref
  32.1 0.0 copy-start
  32.1 0.6 copy-done
  32.7 2.5 %pack.1 = (bf16[3,8192,128]{2,1,0:T(8,128)(2,1)}, bf16[8,24,384]{2,1,0:T(8,128)(2,1)}) custom-call(s32[1]{0:T(128)} %bitcast.me_ref, f32[32,8,128]{2,1,0:T(8,128)} %copy-done, f32[2,8,128]{2,1,0:T(8,128)} %get-tuple-element.25.pre_ref, f32[2,8,128]{2,1,0:T(8,128)} %get-tuple-element.26.tr_ref, ...), custom_call_target="tpu_custom_call", output_to_operand_aliasing={{0}: (11, {})} | custom-call | tf_op jit(solution)/shard_map/pack/pallas_call | solution.py:286
  35.3 13.4 %all_to_all.20.got_ref = bf16[8,24,384]{2,1,0:T(8,128)(2,1)} all-to-all(bf16[8,24,384]{2,1,0:T(8,128)(2,1)} %get-tuple-element.33), channel_id=1, replica_groups=mesh['fluid'=8,'solid'=4] {'fluid'}, dimensions={0} | all-to-all | bytes 294912 | tf_op jit(solution)/shard_map/all_to_all | solution.py:524
  48.7 1.8 %place.1 = (f32[3,32,128]{2,1,0:T(8,128)}, f32[64,64]{1,0:T(8,128)}, f32[8,128]{1,0:T(8,128)}, f32[24,128]{1,0:T(8,128)}, f32[24,128]{1,0:T(8,128)}) custom-call(bf16[8,24,384]{2,1,0:T(8,128)(2,1)} %all_to_all.20.got_ref, f32[3,32,128]{2,1,0:T(8,128)} %bitcast.27, f32[32,128]{1,0:T(8,128)} %stiff_ref.3), custom_call_target="tpu_custom_call" | custom-call | tf_op jit(solution)/shard_map/place/pallas_call | solution.py:336
  50.5 1.3 %collective-permute-start = (f32[24,128]{1,0:T(8,128)}, f32[24,128]{1,0:T(8,128)S(1)}, u32[]{:S(2)}, u32[]{:S(2)}) collective-permute-start(f32[24,128]{1,0:T(8,128)} %get-tuple-element.35), channel_id=1, source_target_pairs={{0,1},{1,2},{2,3},{3,4},{4,5},{5,6},{6,7},{7,8},{8,9},{9,10},{10,1... | collective-permute-start | bytes 36872 | tf_op jit(solution)/shard_map/ppermute | solution.py:526
  51.7 1.3 %collective-permute-start.1 = (f32[24,128]{1,0:T(8,128)}, f32[24,128]{1,0:T(8,128)S(1)}, u32[]{:S(2)}, u32[]{:S(2)}) collective-permute-start(f32[24,128]{1,0:T(8,128)} %get-tuple-element.36), channel_id=1, source_target_pairs={{1,0},{2,1},{3,2},{4,3},{5,4},{6,5},{7,6},{8,7},{9,8},{10,9},{11,1... | collective-permute-start | bytes 36872 | tf_op jit(solution)/shard_map/ppermute | solution.py:527
  53.0 0.8 copy.17
  53.9 0.8 fusion.3
  54.7 5.8 %cholesky.17 = f32[64,64]{1,0:T(8,128)S(1)} custom-call(f32[64,64]{1,0:T(8,128)S(1)} %fusion.3), custom_call_target="Cholesky" | custom-call | tf_op jit(solution)/shard_map/jit(cholesky)/cholesky | solution.py:528
  60.5 0.6 compare_reduce_fusion
  61.2 0.7 fusion
  61.8 4.9 %custom-call.7 = f32[1,64,64]{1,2,0:T(8,128)S(1)} custom-call(f32[1,64,64]{2,1,0:T(8,128)S(1)} %fusion), custom_call_target="InvertDiagBlocksLowerTriangular" | custom-call | tf_op jit(solution)/shard_map/jit(_solve_triangular)/triangular_solve | solution.py:529
  66.7 0.0 collective-permute-done.before_ref
  66.8 0.0 copy-start.4
  66.8 0.0 collective-permute-done.1.after_ref
  66.8 0.0 copy-start.5
  66.8 0.6 copy-done.4
  67.4 0.0 copy-done.5
  67.4 3.4 %sweeps.1 = (f32[3,32,128]{2,1,0:T(8,128)}, f32[32,1,128]{2,1,0:T(1,128)}) custom-call(s32[1]{0:T(128)} %bitcast.me_ref, f32[3,32,128]{2,1,0:T(8,128)} %get-tuple-element.34.force_ref, f32[3,32,128]{2,1,0:T(8,128)} %bitcast.28, f32[32,128]{1,0:T(8,128)} %stiff_ref.3, f32[24,128]{1,0:T(8,128)} %copy-done.4, f32[24,128]{1,0:T(8,128)} %copy-done.5, ...), custom_call_target="tpu_custom_call" | custom-call | tf_op jit(solution)/shard_map/sweeps/pallas_call | solution.py:407
  70.8 5.8 %all-to-all-start.2 = ((f32[32,1,128]{2,1,0:T(1,128)}), f32[32,1,128]{2,1,0:T(1,128)S(1)}, u32[]{:S(2)}, u32[]{:S(2)}) async-start(f32[32,1,128]{2,1,0:T(1,128)} %get-tuple-element.37), calls=%async_computation.2 | async-start | bytes 32768 | tf_op jit(solution)/shard_map/all_to_all | solution.py:531
  76.6 0.2 fusion.1.inv_ref
  76.8 0.0 copy-start.2
  76.8 0.7 copy.18
  77.5 6.2 %all-to-all-done.2.got_ref = f32[32,1,128]{2,1,0:T(1,128)S(1)} async-done(((f32[32,1,128]{2,1,0:T(1,128)}), f32[32,1,128]{2,1,0:T(1,128)S(1)}, u32[]{:S(2)}, u32[]{:S(2)}) %all-to-all-start.2) | async-done | bytes 16416 | tf_op jit(solution)/shard_map/all_to_all | solution.py:531
  83.7 0.0 copy-start.3
  83.7 0.0 copy-done.2
  83.7 0.6 copy-done.3
  84.3 3.3 %update.1 = (f32[3,32,128]{2,1,0:T(8,128)}, bf16[8,16,384]{2,1,0:T(8,128)(2,1)}, f32[1,128]{1,0:T(1,128)}) custom-call(f32[32,1,128]{2,1,0:T(1,128)} %copy-done.3, f32[64,64]{1,0:T(8,128)} %copy-done.2, f32[64,64]{1,0:T(8,128)} %bitcast.29, f32[64,96,128]{2,1,0:T(8,128)} %bitcast.26, f32[3,32,128]{2,1,0:T(8,128)} %get-tuple-element.39.solved_ref, ...), custom_call_target="tpu_custom_call" | custom-call | tf_op jit(solution)/shard_map/update/pallas_call | solution.py:445
  87.6 3.4 %all-to-all-start.3 = ((bf16[8,16,384]{2,1,0:T(8,128)(2,1)}), bf16[8,16,384]{2,1,0:T(8,128)(2,1)S(1)}, u32[]{:S(2)}, u32[]{:S(2)}) async-start(bf16[8,16,384]{2,1,0:T(8,128)(2,1)} %get-tuple-element.42), calls=%async_computation.3 | async-start | bytes 196608 | tf_op jit(solution)/shard_map/all_to_all | solution.py:533
  91.0 1.3 %slice.23 = f32[1,1]{1,0:T(1,128)} slice(f32[1,128]{1,0:T(1,128)} %get-tuple-element.43), slice={[0:1], [64:65]} | slice | bytes 8 | tf_op jit(solution)/shard_map/slice | solution.py:535
  93.0 5.1 %all-to-all-done.3.got_ref = bf16[8,16,384]{2,1,0:T(8,128)(2,1)S(1)} async-done(((bf16[8,16,384]{2,1,0:T(8,128)(2,1)}), bf16[8,16,384]{2,1,0:T(8,128)(2,1)S(1)}, u32[]{:S(2)}, u32[]{:S(2)}) %all-to-all-start.3) | async-done | bytes 98336 | tf_op jit(solution)/shard_map/all_to_all | solution.py:533
  98.1 0.0 copy-start.1
  98.1 0.6 copy-done.1
  98.7 3.7 %wall.1 = f32[3,8192]{1,0:T(4,128)} custom-call(bf16[8,16,384]{2,1,0:T(8,128)(2,1)} %copy-done.1, bf16[128,64]{1,0:T(8,128)(2,1)} %get-tuple-element.29.chosen_ref, bf16[64,128,128]{2,1,0:T(8,128)(2,1)} %rbf_ref.3), custom_call_target="tpu_custom_call" | custom-call | tf_op jit(solution)/shard_map/wall/pallas_call | solution.py:471
  (1 shorter events, 0.0 us)
Async XLA Ops:
  8.0 24.0 %all-to-all-start = ((f32[32,8,128]{2,1,0:T(8,128)}), f32[32,8,128]{2,1,0:T(8,128)S(1)}, u32[]{:S(2)}, u32[]{:S(2)}) async-start(f32[32,8,128]{2,1,0:T(8,128)} %get-tuple-element.24), calls=%async_computation | async-start | bytes 262144 | tf_op jit(solution)/shard_map/all_to_all | solution.py:515
  32.1 0.7 copy-start
  50.5 16.3 %collective-permute-start = (f32[24,128]{1,0:T(8,128)}, f32[24,128]{1,0:T(8,128)S(1)}, u32[]{:S(2)}, u32[]{:S(2)}) collective-permute-start(f32[24,128]{1,0:T(8,128)} %get-tuple-element.35), channel_id=1, source_target_pairs={{0,1},{1,2},{2,3},{3,4},{4,5},{5,6},{6,7},{7,8},{8,9},{9,10},{10,1... | collective-permute-start | bytes 36872 | tf_op jit(solution)/shard_map/ppermute | solution.py:526
  51.7 15.0 %collective-permute-start.1 = (f32[24,128]{1,0:T(8,128)}, f32[24,128]{1,0:T(8,128)S(1)}, u32[]{:S(2)}, u32[]{:S(2)}) collective-permute-start(f32[24,128]{1,0:T(8,128)} %get-tuple-element.36), channel_id=1, source_target_pairs={{1,0},{2,1},{3,2},{4,3},{5,4},{6,5},{7,6},{8,7},{9,8},{10,9},{11,1... | collective-permute-start | bytes 36872 | tf_op jit(solution)/shard_map/ppermute | solution.py:527
  66.8 0.6 copy-start.4
  66.8 0.6 copy-start.5
  70.8 12.9 %all-to-all-start.2 = ((f32[32,1,128]{2,1,0:T(1,128)}), f32[32,1,128]{2,1,0:T(1,128)S(1)}, u32[]{:S(2)}, u32[]{:S(2)}) async-start(f32[32,1,128]{2,1,0:T(1,128)} %get-tuple-element.37), calls=%async_computation.2 | async-start | bytes 32768 | tf_op jit(solution)/shard_map/all_to_all | solution.py:531
  76.8 6.9 %copy-start.2 = (f32[64,64]{1,0:T(8,128)}, f32[64,64]{1,0:T(8,128)S(1)}, u32[]{:S(2)}) copy-start(f32[64,64]{1,0:T(8,128)S(1)} %fusion.1.inv_ref) | copy-start | bytes 49156
  83.7 0.6 copy-start.3
  87.6 10.4 %all-to-all-start.3 = ((bf16[8,16,384]{2,1,0:T(8,128)(2,1)}), bf16[8,16,384]{2,1,0:T(8,128)(2,1)S(1)}, u32[]{:S(2)}, u32[]{:S(2)}) async-start(bf16[8,16,384]{2,1,0:T(8,128)(2,1)} %get-tuple-element.42), calls=%async_computation.3 | async-start | bytes 196608 | tf_op jit(solution)/shard_map/all_to_all | solution.py:533
  98.1 0.6 copy-start.1

commit v2 on v1

v2 whole, which is shorter than its diff:
```python
import jax
import jax.numpy as jnp
from jax import lax
from jax.experimental import pallas as pl
from jax.experimental.pallas import tpu as pltpu
from jax.sharding import PartitionSpec as P

SWEEPS = 4
AXES = ("fluid", "solid")
LANES = 128
spread_rate = 0.25
f32 = jnp.float32
bf16 = jnp.bfloat16
HIGHEST = lax.Precision.HIGHEST
VMEM = pltpu.MemorySpace.VMEM
SMEM = pltpu.MemorySpace.SMEM
ANY = pl.ANY
PARAMS = pltpu.CompilerParams(vmem_limit_bytes=24 * 2**20)


def up_to(value, step):
    return -(-value // step) * step


def dot(a, b, precision=None):
    return lax.dot_general(a, b, (((1,), (0,)), ((), ())), precision=precision, preferred_element_type=f32)


def dot_nt(a, b, precision=None):
    return lax.dot_general(a, b, (((1,), (1,)), ((), ())), precision=precision, preferred_element_type=f32)


def dot_tn(a, b, precision=None):
    return lax.dot_general(a, b, (((0,), (0,)), ((), ())), precision=precision, preferred_element_type=f32)


def iota(shape, dim):
    return lax.broadcasted_iota(jnp.int32, shape, dim)


def split3(value):
    high = value.astype(bf16)
    rest = value - high.astype(f32)
    middle = rest.astype(bf16)
    low = (rest - middle.astype(f32)).astype(bf16)
    return high, middle, low


def spec(memory):
    return pl.BlockSpec(memory_space=memory)


def largest_divisor(value, most):
    return max(d for d in range(1, most + 1) if value % d == 0)


def in_vmem(value):
    return pltpu.with_memory_space_constraint(value, VMEM)


def in_hbm(value):
    return pltpu.with_memory_space_constraint(value, pltpu.MemorySpace.HBM)


def gram_stage(owner, local_row, history, groups, slots):
    count, lines, _ = history.shape
    blocks = owner.shape[1]
    part = count // groups
    chunk = largest_divisor(lines, 16)
    pitch = lines + 8

    def kernel(owner_hbm, row_hbm, hist_ref, gram_ref, chosen_ref, label_ref, held_ref, owner_ref, row_ref, sems):
        small = [
            pltpu.make_async_copy(owner_hbm, owner_ref, sems.at[lines // chunk]),
            pltpu.make_async_copy(row_hbm, row_ref, sems.at[lines // chunk + 1]),
        ]
        for copy in small:
            copy.start()
        copies = [
            pltpu.make_async_copy(
                hist_ref.at[:, pl.ds(k * chunk, chunk), :], held_ref.at[:, pl.ds(k * chunk, chunk), :], sems.at[k]
            )
            for k in range(lines // chunk)
        ]
        for copy in copies:
            copy.start()
        for copy in small:
            copy.wait()
        owners = owner_ref[...]
        names = jnp.where(owners == iota((groups, blocks), 0), 1.0, 0.0)
        before = jnp.where(iota((blocks, blocks), 0) < iota((blocks, blocks), 1), 1.0, 0.0)
        earlier = dot(names.astype(bf16), before.astype(bf16))
        numbers = (row_ref[...] + 1).astype(f32)
        place = iota((slots, blocks), 0).astype(f32)
        for g in range(groups):
            mine = jnp.where((earlier[g : g + 1] == place) & (names[g : g + 1] > 0.5), 1.0, 0.0)
            chosen_ref[g * slots : (g + 1) * slots, :] = mine.astype(bf16)
        labels = dot_nt(jnp.broadcast_to(numbers, (8, blocks)).astype(bf16), chosen_ref[...])
        for g in range(groups):
            label_ref[g : g + 1, :] = jnp.concatenate(
                [labels[0:1, g * slots : (g + 1) * slots], jnp.zeros((1, LANES - slots), f32)], axis=1
            )
        flat = held_ref.reshape(count * pitch, LANES)
        acc = None
        for k in range(lines // chunk):
            copies[k].wait()
            cut = [flat[pl.ds(k * chunk + i, count, stride=pitch), :] for i in range(chunk)]
            parts = split3(jnp.concatenate(cut, axis=1))
            left = jnp.concatenate(parts, axis=0)
            right = jnp.concatenate(parts + (jnp.zeros_like(parts[0]),), axis=0)
            prod = dot_nt(left, right)
            acc = prod if acc is None else acc + prod
        total = acc[0:count, :] + acc[count : 2 * count, :] + acc[2 * count :, :]
        wide = total[:, :LANES] + total[:, LANES:]
        wide = wide + pltpu.roll(wide, LANES // 2, 1)
        pieces = split3(wide)
        for g in range(groups):
            for k in range(3):
                cut = pieces[k][g * part : (g + 1) * part, :]
                if part < 8:
                    cut = jnp.concatenate([cut.astype(f32), jnp.zeros((8 - part, LANES), f32)], axis=0).astype(bf16)
                gram_ref[g, :, k * LANES : (k + 1) * LANES] = cut

    return pl.pallas_call(
        kernel,
        out_shape=(
            VMEM((groups, 8, 3 * LANES), bf16),
            VMEM((groups * slots, blocks), bf16),
            VMEM((groups, LANES), f32),
        ),
        in_specs=[spec(ANY), spec(ANY), spec(ANY)],
        out_specs=(spec(VMEM), spec(VMEM), spec(VMEM)),
        scratch_shapes=[
            pltpu.VMEM((count, pitch, LANES), f32),
            pltpu.VMEM(owner.shape, jnp.int32),
            pltpu.VMEM(owner.shape, jnp.int32),
            pltpu.SemaphoreType.DMA((lines // chunk + 2,)),
        ],
        name="gram",
        compiler_params=PARAMS,
    )(in_hbm(owner), in_hbm(local_row), in_hbm(history))


def flow_stage(flow, head, tail, wall_motion, normal_operator, coupling, stencil, rbf, chosen, labels, gram, tile, slots, capacity):
    comps, points, normal = flow.shape
    groups = gram.shape[0]
    blocks = rbf.shape[0]
    steps = points // tile
    inside = tile // LANES
    names = comps * inside

    def kernel(flow_hbm, head_ref, tail_ref, motion_hbm, op_hbm, coup_hbm, sten_hbm, rbf_hbm, chosen_ref, label_ref, gram_ref, new_hbm, send_ref, held, fresh_ref, motion_ref, op_ref, coup_ref, sten_ref, rbf_ref, cols, turns, maps, quarter, outer, points_ref, sems, into, out):
        small = [
            pltpu.make_async_copy(coup_hbm, coup_ref, sems.at[0]),
            pltpu.make_async_copy(motion_hbm, motion_ref, sems.at[1]),
            pltpu.make_async_copy(op_hbm, op_ref, sems.at[2]),
            pltpu.make_async_copy(sten_hbm, sten_ref, sems.at[3]),
        ]
        rbf_copy = pltpu.make_async_copy(rbf_hbm, rbf_ref, sems.at[4])

        def load(t):
            at = pl.ds(pl.multiple_of(t * tile, tile), tile)
            return pltpu.make_async_copy(flow_hbm.at[:, at, :], held.at[:, at, :], into.at[t])

        def store(t):
            at = pl.ds(pl.multiple_of(t * tile, tile), tile)
            return pltpu.make_async_copy(fresh_ref.at[:, at, :], new_hbm.at[:, at, :], out.at[t])

        for copy in small:
            copy.start()
        load(0).start()
        load(1).start()
        rbf_copy.start()
        for t in range(2, steps):
            load(t).start()
        small[0].wait()
        high, middle, _ = split3(coup_ref[...])
        rows = iota((LANES, LANES), 0)
        value = jnp.where(rows < 2 * names, high.astype(f32), 0.0)
        value = jnp.where((rows >= 2 * names) & (rows < 3 * names), middle.astype(f32), value)
        value = jnp.where((rows >= 3 * names) & (rows < 4 * names), high.astype(f32), value)
        value = jnp.where((rows >= 4 * names) & (rows < 5 * names), middle.astype(f32), value)
        for copy in small[1:]:
            copy.wait()
        outer[0:normal, :] = op_ref[...]
        outer[normal:, :] = value.astype(bf16)
        which = lax.rem(iota((1, LANES), 1), names)
        sten = sten_ref[...].astype(f32)
        eye = iota((LANES, LANES), 0) == iota((LANES, LANES), 1)
        points_ref[...] = jnp.zeros(points_ref.shape, f32)
        for t in range(steps):
            for c in range(comps):
                for j in range(inside):
                    o = t * tile + j * LANES
                    cols[t, c * inside + j : c * inside + j + 1, :] = motion_ref[c : c + 1, o : o + LANES]
            high, middle, low = [piece.astype(f32) for piece in split3(cols[t, 0:names, :])]
            parts = [high, middle, high, low, middle, jnp.zeros((LANES - 5 * names, LANES), f32)]
            turns[t] = jnp.transpose(jnp.concatenate(parts, axis=0)).astype(bf16)
        load(0).wait()
        rbf_copy.wait()

        def mapping(first):
            for j in range(inside):
                got = dot(points_ref[first + j].astype(bf16), rbf_ref[first + j])
                for c in range(comps):
                    maps[c, pl.ds(first + j, 1), :] = got[c : c + 1, :]

        def step(i, carry, ahead=True):
            base = pl.multiple_of(i * tile, tile)
            if ahead:
                load(i + 1).wait()
            mapping(jnp.maximum(i - 1, 0) * inside)
            turned = turns[i]
            before = pl.multiple_of(jnp.maximum(base - 16, 0), 16)
            after = pl.multiple_of(jnp.minimum(base + tile, points - 16), 16)
            for c in range(comps):
                above = jnp.where(i > 0, held[c, pl.ds(before, 16), :].astype(f32)[15:16, :], tail_ref[c].astype(f32))
                below = jnp.where(i < steps - 1, held[c, pl.ds(after, 16), :].astype(f32)[0:1, :], head_ref[c].astype(f32))
                quarter[c, 7:8, :] = above * spread_rate
                quarter[c, 8 + tile : 9 + tile, :] = below * spread_rate
                quarter[c, 8 : 8 + tile, :] = held[c, pl.ds(base, tile), :].astype(f32) * spread_rate
                motion = [turned * jnp.where(which == c * inside + j, 1.0, 0.0).astype(bf16) for j in range(inside)]
                moved = dot(jnp.concatenate([held[c, pl.ds(base, tile), :], jnp.concatenate(motion, axis=0)], axis=1), outer[...])
                for j in range(inside):
                    o = j * LANES
                    at = pl.ds(pl.multiple_of(base + o, LANES), LANES)
                    fresh = moved[o : o + LANES, :]
                    mid = quarter[c, 8 + o : 8 + o + LANES, :]
                    around = quarter[c, 7 + o : 7 + o + LANES, :] + quarter[c, 9 + o : 9 + o + LANES, :]
                    fresh = (fresh + ((mid + mid) + around)).astype(bf16)
                    fresh_ref[c, at, :] = fresh
                    point = jnp.sum(fresh.astype(f32) * sten, axis=1, keepdims=True)
                    points_ref[i * inside + j, c : c + 1, :] = jnp.sum(jnp.where(eye, point, 0.0), axis=0, keepdims=True)
            store(i).start()
            return carry

        lax.fori_loop(0, steps - 1, step, 0)
        step(steps - 1, 0, ahead=False)
        mapping((steps - 1) * inside)
        label_row = iota((slots, LANES), 0) == capacity
        for g in range(groups):
            send_ref[g, slots : slots + 8, :] = gram_ref[g]
        for c in range(comps):
            out_c = dot(chosen_ref[...], maps[c].astype(bf16))
            for g in range(groups):
                cut = out_c[g * slots : (g + 1) * slots, :]
                if c == 0:
                    cut = jnp.where(label_row, label_ref[g : g + 1, :], cut)
                send_ref[g, 0:slots, c * LANES : (c + 1) * LANES] = cut.astype(bf16)
        for t in range(steps):
            store(t).wait()

    return pl.pallas_call(
        kernel,
        out_shape=(
            jax.ShapeDtypeStruct(flow.shape, bf16),
            VMEM((groups, slots + 8, comps * LANES), bf16),
        ),
        in_specs=[spec(ANY), spec(VMEM), spec(VMEM)] + [spec(ANY)] * 5 + [spec(VMEM)] * 3,
        out_specs=(spec(ANY), spec(VMEM)),
        scratch_shapes=[
            pltpu.VMEM(flow.shape, bf16),
            pltpu.VMEM(flow.shape, bf16),
            pltpu.VMEM(wall_motion.shape, f32),
            pltpu.VMEM(normal_operator.shape, bf16),
            pltpu.VMEM(coupling.shape, f32),
            pltpu.VMEM(stencil.shape, bf16),
            pltpu.VMEM(rbf.shape, bf16),
            pltpu.VMEM((steps, names, LANES), f32),
            pltpu.VMEM((steps, LANES, LANES), bf16),
            pltpu.VMEM((comps, blocks, LANES), f32),
            pltpu.VMEM((comps, tile + 16, LANES), f32),
            pltpu.VMEM((2 * LANES, LANES), bf16),
            pltpu.VMEM((blocks, 8, LANES), f32),
            pltpu.SemaphoreType.DMA((5,)),
            pltpu.SemaphoreType.DMA((steps,)),
            pltpu.SemaphoreType.DMA((steps,)),
        ],
        name="flow",
        compiler_params=PARAMS,
    )(in_hbm(flow), in_vmem(head), in_vmem(tail), in_hbm(wall_motion), in_hbm(normal_operator), in_hbm(coupling), in_hbm(stencil), in_hbm(rbf), in_vmem(chosen), in_vmem(labels), in_vmem(gram))


def place_stage(arrived, displacement, stiffness, slots, capacity, count):
    comps, rows, width = displacement.shape
    groups = arrived.shape[0]
    part = count // groups
    half = part // 2
    depth = SWEEPS
    short = depth - 1

    def kernel(got_ref, disp_ref, stiff_ref, force_ref, gram_ref, label_ref, head_ref, tail_ref):
        index = iota((rows, slots), 0).astype(f32) + 1.0
        total = jnp.zeros((rows, comps * width), f32)
        extra = jnp.zeros((8, 3 * LANES), f32)
        for g in range(groups):
            labels = got_ref[g, capacity : capacity + 1, 0:LANES].astype(f32)
            label_ref[g : g + 1, :] = labels
            placed = jnp.where(labels[:, 0:slots] == index, 1.0, 0.0).astype(bf16)
            total = total + dot(placed, got_ref[g, 0:slots, :])
            extra = extra + got_ref[g, slots : slots + 8, :].astype(f32)
        for c in range(comps):
            force_ref[c] = total[:, c * width : (c + 1) * width]
        gram = extra[:, 0:LANES] + extra[:, LANES : 2 * LANES] + extra[:, 2 * LANES : 3 * LANES]
        lower = pltpu.roll(gram, 8 - half, 0)
        gram_ref[...] = jnp.where(iota((8, LANES), 1) < LANES // 2, gram, lower)
        for c in range(comps):
            head_ref[c * short : (c + 1) * short, :] = total[0:short, c * width : (c + 1) * width]
            tail_ref[c * short : (c + 1) * short, :] = total[rows - short : rows, c * width : (c + 1) * width]
            at = comps * short + c * depth
            head_ref[at : at + depth, :] = disp_ref[c, 0:depth, :]
            tail_ref[at : at + depth, :] = disp_ref[c, rows - depth : rows, :]
        at = comps * (short + depth)
        head_ref[at : at + short, :] = stiff_ref[0:short, :]
        tail_ref[at : at + short, :] = stiff_ref[rows - short : rows, :]

    edge = (comps * (short + depth) + short, width)
    return pl.pallas_call(
        kernel,
        out_shape=(
            VMEM((comps, rows, width), f32),
            VMEM((8, LANES), f32),
            VMEM((groups, LANES), f32),
            VMEM(edge, f32),
            VMEM(edge, f32),
        ),
        name="place",
        compiler_params=PARAMS,
    )(in_vmem(arrived), in_vmem(displacement), in_vmem(stiffness))


def sweep_stage(me, force, displacement, stiffness, before, after, held, gram, half, devices):
    comps, rows, width = displacement.shape
    count = held.shape[0]
    depth = SWEEPS
    short = depth - 1
    rim = 8
    whole = rows + 2 * rim

    def kernel(me_ref, force_ref, disp_ref, stiff_ref, before_ref, after_ref, hist_ref, gram_ref, solved_ref, send_ref, ext, sums):
        own = me_ref[0]
        row = iota((whole, width), 0)
        lane = iota((whole, width), 1)
        lowest = jnp.where(own > 0, rim - depth, rim)
        highest = jnp.where(own < devices - 1, rim + rows + depth, rim + rows)
        valid = jnp.where((row >= lowest) & (row < highest), 1.0, 0.0)
        at = comps * (short + depth)
        ext[...] = jnp.zeros(ext.shape, f32)
        ext[0, rim - short : rim, :] = before_ref[at : at + short, :]
        ext[0, rim : rim + rows, :] = stiff_ref[...]
        ext[0, rim + rows : rim + rows + short, :] = after_ref[at : at + short, :]
        scale = valid / (4.0 + ext[0])
        left_ok = jnp.where(lane > 0, 1.0, 0.0)
        right_ok = jnp.where(lane < width - 1, 1.0, 0.0)
        squares = jnp.zeros((8, width), f32)
        residuals = []
        for c in range(comps):
            f = 1 + 2 * c
            ext[f, rim - short : rim, :] = before_ref[c * short : (c + 1) * short, :]
            ext[f, rim : rim + rows, :] = force_ref[c]
            ext[f, rim + rows : rim + rows + short, :] = after_ref[c * short : (c + 1) * short, :]
            d = comps * short + c * depth
            ext[f + 1, rim - depth : rim, :] = before_ref[d : d + depth, :]
            ext[f + 1, rim : rim + rows, :] = disp_ref[c]
            ext[f + 1, rim + rows : rim + rows + depth, :] = after_ref[d : d + depth, :]
        push = [ext[1 + 2 * c] for c in range(comps)]
        solved = [ext[2 + 2 * c] for c in range(comps)]
        for sweep in range(SWEEPS):
            for c in range(comps):
                old = solved[c]
                beside = pltpu.roll(old, 1, 0) + pltpu.roll(old, whole - 1, 0)
                beside = beside + pltpu.roll(old, 1, 1) * left_ok + pltpu.roll(old, width - 1, 1) * right_ok
                solved[c] = (push[c] + beside) * scale
        for c in range(comps):
            mine = solved[c][rim : rim + rows, :]
            solved_ref[c] = mine
            residual = mine - disp_ref[c]
            residuals.append(residual)
            square = residual * residual
            for k in range(rows // 8):
                squares = squares + square[8 * k : 8 * k + 8, :]
        sums[count:, :] = jnp.zeros((LANES - count, width), f32)
        sums[count : count + 1, :] = jnp.sum(squares, axis=0, keepdims=True)
        flat = jnp.concatenate(residuals, axis=0)
        for j in range(count):
            prod = hist_ref[j, 0 : comps * rows, :] * flat
            sums[j : j + 1, :] = jnp.sum(prod, axis=0, keepdims=True)
        line = dot_nt(jnp.ones((8, width), f32), sums[...], HIGHEST)
        chunk = jnp.where(iota((8, LANES), 0) < half, gram_ref[...], line)
        for d in range(devices):
            send_ref[d] = chunk

    return pl.pallas_call(
        kernel,
        out_shape=(
            VMEM((comps, rows, width), f32),
            VMEM((devices, 8, LANES), f32),
        ),
        in_specs=[spec(SMEM)] + [spec(VMEM)] * 7,
        out_specs=(spec(VMEM), spec(VMEM)),
        scratch_shapes=[pltpu.VMEM((1 + 2 * comps, whole, width), f32), pltpu.VMEM((LANES, width), f32)],
        name="sweeps",
        compiler_params=PARAMS,
    )(me, in_vmem(force), in_vmem(displacement), in_vmem(stiffness), in_vmem(before), in_vmem(after), in_vmem(held), in_vmem(gram))


def eliminate(rows):
    sub = iota((8, LANES), 0)
    number = len(rows)
    for p in range(number):
        cols = [[jnp.broadcast_to(rows[v][:, 8 * p + i : 8 * p + i + 1], (8, LANES)) for i in range(8)] for v in range(number)]
        pivot = rows[p]
        diag = list(cols[p])
        for i in range(8):
            inverse = 1.0 / diag[i][i : i + 1, :]
            factor = jnp.where(sub == i, 0.0, diag[i])
            line = pivot[i : i + 1, :] * inverse
            pivot = jnp.where(sub == i, line, pivot) - factor * line
            for j in range(i + 1, 8):
                edge = diag[j][i : i + 1, :] * inverse
                diag[j] = jnp.where(sub == i, edge, diag[j]) - factor * edge
        for v in range(number):
            if v != p:
                value = rows[v]
                for i in range(8):
                    value = value - cols[v][i] * pivot[i : i + 1, :]
                rows[v] = value
        rows[p] = pivot
    return rows


def update_stage(arrived, history, solved, labels, count, slots):
    comps, rows, width = solved.shape
    lines = history.shape[1]
    groups = labels.shape[0]
    devices = arrived.shape[0]
    inner = devices // groups
    part = count // groups
    half = part // 2

    def kernel(got_ref, hist_hbm, solved_ref, label_ref, next_ref, reply_ref, line_ref, table, coeff, hist_ref, sem):
        fetch = pltpu.make_async_copy(hist_hbm, hist_ref, sem)
        fetch.start()
        line = got_ref[0]
        for d in range(1, devices):
            line = line + got_ref[d]
        line = line[half : half + 1, :]
        line_ref[...] = line
        for g in range(groups):
            packed = got_ref[g * inner]
            for s in range(1, inner):
                packed = packed + got_ref[g * inner + s]
            table[g * part : g * part + half, :] = packed[0:half, :]
            table[g * part + half : (g + 1) * part, :] = pltpu.roll(packed, LANES // 2, 1)[0:half, :]
        lane = iota((8, LANES), 1)
        sub = iota((8, LANES), 0)
        system = []
        for v in range(count // 8):
            own = jnp.sum(jnp.where(lane == sub + 8 * v, line, 0.0), axis=1, keepdims=True)
            value = jnp.where(lane < count, table[8 * v : 8 * v + 8, :], 0.0)
            system.append(jnp.where(lane == count, -own, value))
        system = eliminate(system)
        for v in range(count // 8):
            coeff[8 * v : 8 * v + 8, :] = jnp.broadcast_to(system[v][:, count : count + 1], (8, LANES))

        fetch.wait()

        def body(j, total):
            return total + hist_ref[j] * coeff[pl.ds(j, 1), :]

        update = lax.fori_loop(0, count, body, jnp.zeros((lines, width), f32), unroll=8)
        shell = []
        for c in range(comps):
            fresh = solved_ref[c] + update[c * rows : (c + 1) * rows, :]
            next_ref[c] = fresh
            shell.append(fresh.astype(bf16))
        shell = jnp.concatenate(shell, axis=1)
        index = iota((rows, slots), 0).astype(f32) + 1.0
        for g in range(groups):
            placed = jnp.where(label_ref[g : g + 1, 0:slots] == index, 1.0, 0.0).astype(bf16)
            reply_ref[g] = dot_tn(placed, shell).astype(bf16)

    return pl.pallas_call(
        kernel,
        out_shape=(
            VMEM((comps, rows, width), f32),
            VMEM((groups, slots, comps * width), bf16),
            VMEM((1, LANES), f32),
        ),
        in_specs=[spec(VMEM), spec(ANY), spec(VMEM), spec(VMEM)],
        scratch_shapes=[
            pltpu.VMEM((count, LANES), f32),
            pltpu.VMEM((count, width), f32),
            pltpu.VMEM((count, lines, width), f32),
            pltpu.SemaphoreType.DMA,
        ],
        name="update",
        compiler_params=PARAMS,
    )(in_vmem(arrived), in_hbm(history), in_vmem(solved), in_vmem(labels))


def wall_stage(returned, chosen, rbf, comps):
    blocks, block, width = rbf.shape
    groups, slots, _ = returned.shape

    pieces = largest_divisor(blocks, 4)
    each = blocks // pieces

    def kernel(got_ref, chosen_ref, rbf_hbm, out_hbm, shells, rbf_ref, out_ref, sems, outs):
        copies = [
            pltpu.make_async_copy(rbf_hbm.at[pl.ds(k * each, each)], rbf_ref.at[pl.ds(k * each, each)], sems.at[k])
            for k in range(pieces)
        ]
        for copy in copies:
            copy.start()
        wide = each * block
        stores = [
            pltpu.make_async_copy(
                out_ref.at[:, pl.ds(k * wide, wide)], out_hbm.at[:, pl.ds(k * wide, wide)], outs.at[k]
            )
            for k in range(pieces)
        ]
        got = jnp.concatenate([got_ref[g] for g in range(groups)], axis=0)
        fetched = dot_tn(chosen_ref[...], got)
        for c in range(comps):
            shells[:, c, :] = fetched[:, c * width : (c + 1) * width]
        for k in range(pieces):
            copies[k].wait()
            for b in range(k * each, (k + 1) * each):
                res = dot_nt(shells[b].astype(bf16), rbf_ref[b])
                out_ref[:, b * block : (b + 1) * block] = res[0:comps, :]
            stores[k].start()
        for copy in stores:
            copy.wait()

    return pl.pallas_call(
        kernel,
        out_shape=jax.ShapeDtypeStruct((comps, blocks * block), f32),
        in_specs=[spec(VMEM), spec(VMEM), spec(ANY)],
        out_specs=spec(ANY),
        scratch_shapes=[
            pltpu.VMEM((blocks, 8, width), f32),
            pltpu.VMEM(rbf.shape, bf16),
            pltpu.VMEM((comps, blocks * block), f32),
            pltpu.SemaphoreType.DMA((pieces,)),
            pltpu.SemaphoreType.DMA((pieces,)),
        ],
        name="wall",
        compiler_params=PARAMS,
    )(in_vmem(returned), in_vmem(chosen), in_hbm(rbf))


def per_device(
    flow,
    wall_motion,
    normal_operator,
    wall_coupling,
    wall_stencil,
    rbf_blocks,
    block_owner,
    block_row,
    displacement,
    stiffness,
    residual_history,
    solution_history,
):
    groups = lax.axis_size("fluid")
    devices = groups * lax.axis_size("solid")
    comps, points, normal = flow.shape
    blocks, block, width = rbf_blocks.shape
    count = residual_history.shape[0]
    rows = displacement.shape[0]
    capacity = max(2, (3 * blocks + 2 * groups - 1) // (2 * groups))
    slots = up_to(capacity + 1, 16)
    me = lax.axis_index(AXES).astype(jnp.int32).reshape(1)
    up = [(i, i + 1) for i in range(devices - 1)]
    down = [(i + 1, i) for i in range(devices - 1)]

    disp = displacement.transpose(1, 0, 2)
    res_hist = residual_history.transpose(0, 2, 1, 3).reshape(count, comps * rows, width)
    sol_hist = solution_history.transpose(0, 2, 1, 3).reshape(count, comps * rows, width)
    owner = block_owner.reshape(1, blocks)
    local_row = block_row.reshape(1, blocks)
    coupling = wall_coupling.reshape(1, normal)
    stencil = wall_stencil.reshape(1, normal)

    flow_tail = lax.ppermute(flow[:, points - 1 :, :], AXES, up)
    flow_head = lax.ppermute(flow[:, :1, :], AXES, down)
    gram, chosen, labels = gram_stage(owner, local_row, res_hist, groups, slots)
    tile = 1024 if points % 1024 == 0 else points
    new_flow, send = flow_stage(
        flow, flow_head, flow_tail, wall_motion, normal_operator, coupling, stencil, rbf_blocks, chosen, labels, gram,
        tile, slots, capacity,
    )
    arrived = lax.all_to_all(send, "fluid", 0, 0, tiled=True)
    force, gram, placed_labels, head, tail = place_stage(arrived, disp, stiffness, slots, capacity, count)
    before = lax.ppermute(tail, AXES, up)
    after = lax.ppermute(head, AXES, down)
    half = count // groups // 2
    solved, send = sweep_stage(me, force, disp, stiffness, before, after, res_hist, gram, half, devices)
    got = lax.all_to_all(send, AXES, 0, 0, tiled=True)
    fresh, reply, line = update_stage(got, sol_hist, solved, placed_labels, count, slots)
    returned = lax.all_to_all(reply, "fluid", 0, 0, tiled=True)
    wall_next = wall_stage(returned, chosen, rbf_blocks, comps)
    return (new_flow, fresh.transpose(1, 0, 2), wall_next, jnp.sqrt(line[0, count]))


def solution(mesh):
    return jax.shard_map(
        per_device,
        mesh=mesh,
        in_specs=(
            P(None, ("fluid", "solid"), None),
            P(None, ("fluid", "solid")),
            P(),
            P(),
            P(),
            P(("fluid", "solid"), None, None),
            P(("fluid", "solid"), None),
            P(("fluid", "solid"), None),
            P(("fluid", "solid"), None, None),
            P(("fluid", "solid"), None),
            P(None, ("fluid", "solid"), None, None),
            P(None, ("fluid", "solid"), None, None),
        ),
        out_specs=(
            P(None, ("fluid", "solid"), None),
            P(("fluid", "solid"), None, None),
            P(None, ("fluid", "solid")),
            P(),
        ),
        check_vma=False,
    )
```

time: 104 us -> 79.4 us (0.76)
  blocking collectives: 13.4 us -> 31.8 us
  other arithmetic: 12.8 us -> 0 us
  Pallas kernels: 37.4 us -> 24.9 us
  starting transfers between devices: 19.1 us -> 9.76 us
  local copies, waits for them, and re-layouts: 6.64 us -> 2.09 us
  waiting for transfers between devices: 11.3 us -> 7.82 us
    all_to_all x0 -> x1, blocking collectives: none -> 14.5 us  [per_device(): got = lax.all_to_all(send, AXES, 0, 0, tiled=True)]
    all_to_all x2 -> x0, starting transfers between devices: 13.1 us -> none  [per_device(): got = lax.all_to_all(send, AXES, 0, 0, tiled=True)]
    pallas_call x6 -> x5, Pallas kernels: 33.8 us -> 21.6 us  [the longest x1 13.3 us: flow_stage(): pl.pallas_call(kernel, out_shape=(jax.ShapeDtypeStruct(flow.shape, bf16),...]
    another operation x5 -> x0, other arithmetic: 12.1 us -> none  [the longest x3 6.52 us: per_device(): lower = jnp.linalg.cholesky(gram)]
    all_to_all x2 -> x0, waiting for transfers between devices: 6.18 us -> none  [per_device(): got = lax.all_to_all(send, AXES, 0, 0, tiled=True)]
    all_to_all x1, blocking collectives: 13.4 us -> 17.3 us  [per_device(): arrived = lax.all_to_all(send, 'fluid', 0, 0, tiled=True)]
    ppermute x2 -> x4, starting transfers between devices: 2.57 us -> 6.39 us  [the longest x1 2.52 us: per_device(): flow_tail = lax.ppermute(flow[:, points - 1:, :], AXES, up)]
    ppermute x2 -> x4, waiting for transfers between devices: 0.02 us -> 2.62 us  [the longest x1 2.61 us: per_device(): after = lax.ppermute(head, AXES, down)]
  transfers between devices with their start and end apart: 5 -> 5, of which waited for: 2 -> 2; matrix products, arithmetic and copies ran while one was open for 15% -> 2% of each run, Pallas kernels for 16% -> 5%
where the time goes in v2:
time: 79.4 us; the launch traced here: 79 us
  blocking collectives  31.8 us (40%)
  Pallas kernels  24.9 us (31%)
  starting transfers between devices  9.76 us (12%)
  waiting for transfers between devices  7.82 us (10%)
  between operations  2.59 us (3%)
  local copies, waits for them, and re-layouts  2.09 us (3%)
    all_to_all x1, blocking collectives, per_device(): arrived = lax.all_to_all(send, 'fluid', 0, 0, tiled=True)  17.3 us
    all_to_all x1, blocking collectives, per_device(): got = lax.all_to_all(send, AXES, 0, 0, tiled=True)  14.5 us
    pallas_call x1, Pallas kernels, flow_stage(): pl.pallas_call(kernel, out_shape=(jax.ShapeDtypeStruct(flow.shape, bf16),...  13.3 us
    all_to_all x1, waiting for transfers between devices, per_device(): returned = lax.all_to_all(reply, 'fluid', 0, 0, tiled=True)  5.2 us
    pallas_call x1, Pallas kernels, gram_stage(): pl.pallas_call(kernel, out_shape=(VMEM((groups, 8, 3 * LANES), bf16), VME...  4.26 us
    all_to_all x1, starting transfers between devices, per_device(): returned = lax.all_to_all(reply, 'fluid', 0, 0, tiled=True)  3.37 us
    pallas_call x1, Pallas kernels, wall_stage(): pl.pallas_call(kernel, out_shape=jax.ShapeDtypeStruct((comps, blocks * bl...  3.28 us
    pallas_call x1, Pallas kernels, update_stage(): pl.pallas_call(kernel, out_shape=(VMEM((comps, rows, width), f32), VMEM((...  3.04 us
  transfers between devices with their start and end apart: 5, of which 2 were waited for; matrix products, arithmetic and copies ran while one was open for 2% of the time, Pallas kernels for 5%

profile of v2, /device:TPU:0, one launch (start us, length us, event | category | flops | bytes accessed | tf_op | source)
XLA Modules:
  0.0 79.0 jit_solution(13494354568279291751)
XLA Ops:
  0.6 0.0 copy-start
  0.6 0.0 copy-start.2
  0.7 0.0 copy-start.1
  0.7 0.9 %fusion = (bf16[3,1,128]{2,1,0:T(2,128)(2,1)S(1)}, bf16[3,1,128]{2,1,0:T(2,128)(2,1)S(1)}) fusion(bf16[3,8192,128]{2,1,0:T(8,128)(2,1)} %flow_hbm.1), kind=kLoop, calls=%fused_computation | loop fusion | bytes 3072 | tf_op jit(solution)/shard_map/slice | solution.py:587
  1.5 2.5 %collective-permute-start.1 = (bf16[3,1,128]{2,1,0:T(2,128)(2,1)S(1)}, bf16[3,1,128]{2,1,0:T(2,128)(2,1)S(1)}, u32[]{:S(2)}, u32[]{:S(2)}) collective-permute-start(bf16[3,1,128]{2,1,0:T(2,128)(2,1)S(1)} %get-tuple-element.34), channel_id=1, source_target_pairs={{0,1},{1,2},{2,3},{3,4},{4,5},{5,6},{6,7},{7,8},{8,9},{9,10},{10,1... | collective-permute-start | bytes 2312 | tf_op jit(solution)/shard_map/ppermute | solution.py:587
  4.1 1.3 %collective-permute-start = (bf16[3,1,128]{2,1,0:T(2,128)(2,1)S(1)}, bf16[3,1,128]{2,1,0:T(2,128)(2,1)S(1)}, u32[]{:S(2)}, u32[]{:S(2)}) collective-permute-start(bf16[3,1,128]{2,1,0:T(2,128)(2,1)S(1)} %get-tuple-element.35), channel_id=1, source_target_pairs={{1,0},{2,1},{3,2},{4,3},{5,4},{6,5},{7,6},{8,7},{9,8},{10,9},{11,1... | collective-permute-start | bytes 2312 | tf_op jit(solution)/shard_map/ppermute | solution.py:588
  5.4 4.3 %gram.1 = (bf16[8,8,384]{2,1,0:T(8,128)(2,1)S(1)}, bf16[128,64]{1,0:T(8,128)(2,1)S(1)}, f32[8,128]{1,0:T(8,128)S(1)}) custom-call(s32[1,64]{1,0:T(1,128)} %bitcast.20, s32[1,64]{1,0:T(1,128)} %bitcast.21, f32[64,96,128]{2,1,0:T(8,128)} %bitcast.15), custom_call_target="tpu_custom_call" | custom-call | tf_op jit(solution)/shard_map/gram/pallas_call | solution.py:124
  9.6 0.0 collective-permute-done.1.tail_ref
  9.6 0.0 collective-permute-done.head_ref
  9.6 13.3 %flow.1 = (bf16[3,8192,128]{2,1,0:T(8,128)(2,1)}, bf16[8,24,384]{2,1,0:T(8,128)(2,1)S(1)}) custom-call(bf16[3,8192,128]{2,1,0:T(8,128)(2,1)} %flow_hbm.1, bf16[3,1,128]{2,1,0:T(2,128)(2,1)S(1)} %collective-permute-done.head_ref, bf16[3,1,128]{2,1,0:T(2,128)(2,1)S(1)} %collective-permute-done.1.tail_ref, f32[3,8192]{1,0:T(4,128)} %motion_hbm.1, ...), custom_call_target="tpu_custom_call" | custom-call | tf_op jit(solution)/shard_map/flow/pallas_call | solution.py:253
  23.0 17.3 %all_to_all.15.got_ref = bf16[8,24,384]{2,1,0:T(8,128)(2,1)S(1)} all-to-all(bf16[8,24,384]{2,1,0:T(8,128)(2,1)S(1)} %get-tuple-element.23), channel_id=1, replica_groups=mesh['fluid'=8,'solid'=4] {'fluid'}, dimensions={0} | all-to-all | bytes 294912 | tf_op jit(solution)/shard_map/all_to_all | solution.py:595
  40.3 0.0 copy-done.2
  40.3 0.0 copy-done.1
  40.3 0.2 place.1
  40.5 1.3 %collective-permute-start.2 = (f32[24,128]{1,0:T(8,128)S(1)}, f32[24,128]{1,0:T(8,128)S(1)}, u32[]{:S(2)}, u32[]{:S(2)}) collective-permute-start(f32[24,128]{1,0:T(8,128)S(1)} %get-tuple-element.25), channel_id=1, source_target_pairs={{0,1},{1,2},{2,3},{3,4},{4,5},{5,6},{6,7},{7,8},{8,9},{9,10},{10,1... | collective-permute-start | bytes 36872 | tf_op jit(solution)/shard_map/ppermute | solution.py:597
  41.8 1.3 %collective-permute-start.3 = (f32[24,128]{1,0:T(8,128)S(1)}, f32[24,128]{1,0:T(8,128)S(1)}, u32[]{:S(2)}, u32[]{:S(2)}) collective-permute-start(f32[24,128]{1,0:T(8,128)S(1)} %get-tuple-element.26), channel_id=1, source_target_pairs={{1,0},{2,1},{3,2},{4,3},{5,4},{6,5},{7,6},{8,7},{9,8},{10,9},{11,1... | collective-permute-start | bytes 36872 | tf_op jit(solution)/shard_map/ppermute | solution.py:598
  43.1 0.0 collective-permute-done.2.before_ref
  43.1 2.6 %collective-permute-done.3.after_ref = f32[24,128]{1,0:T(8,128)S(1)} collective-permute-done((f32[24,128]{1,0:T(8,128)S(1)}, f32[24,128]{1,0:T(8,128)S(1)}, u32[]{:S(2)}, u32[]{:S(2)}) %collective-permute-start.3) | collective-permute-done | bytes 12320 | tf_op jit(solution)/shard_map/ppermute | solution.py:598
  45.7 0.0 copy-done
  45.7 0.8 sweeps.1
  46.5 14.5 %all_to_all.16.got_ref = f32[32,8,128]{2,1,0:T(8,128)S(1)} all-to-all(f32[32,8,128]{2,1,0:T(8,128)S(1)} %get-tuple-element.28), channel_id=1, replica_groups=mesh['fluid'=8,'solid'=4] {'fluid','solid'}, dimensions={0} | all-to-all | bytes 262144 | tf_op jit(solution)/shard_map/all_to_all | solution.py:601
  61.0 3.0 %update.1 = (f32[3,32,128]{2,1,0:T(8,128)S(1)}, bf16[8,16,384]{2,1,0:T(8,128)(2,1)}, f32[1,128]{1,0:T(1,128)S(1)}) custom-call(f32[32,8,128]{2,1,0:T(8,128)S(1)} %all_to_all.16.got_ref, f32[64,96,128]{2,1,0:T(8,128)} %bitcast.19, f32[3,32,128]{2,1,0:T(8,128)S(1)} %get-tuple-element.29.solved_ref, f32[8,128]{1,0:T(8,128)S(1)} %get-tuple-element.30.label_ref), custom_call_target="tpu_custom_call" | custom-call | tf_op jit(solution)/shard_map/update/pallas_call | solution.py:483
  64.1 3.4 %all-to-all-start.2 = ((bf16[8,16,384]{2,1,0:T(8,128)(2,1)}), bf16[8,16,384]{2,1,0:T(8,128)(2,1)S(1)}, u32[]{:S(2)}, u32[]{:S(2)}) async-start(bf16[8,16,384]{2,1,0:T(8,128)(2,1)} %get-tuple-element.32), calls=%async_computation.2 | async-start | bytes 196608 | tf_op jit(solution)/shard_map/all_to_all | solution.py:603
  67.4 0.6 slice.11
  68.7 0.6 copy.16
  69.3 5.2 %all-to-all-done.2.got_ref = bf16[8,16,384]{2,1,0:T(8,128)(2,1)S(1)} async-done(((bf16[8,16,384]{2,1,0:T(8,128)(2,1)}), bf16[8,16,384]{2,1,0:T(8,128)(2,1)S(1)}, u32[]{:S(2)}, u32[]{:S(2)}) %all-to-all-start.2) | async-done | bytes 98336 | tf_op jit(solution)/shard_map/all_to_all | solution.py:603
  74.5 3.3 %wall.1 = f32[3,8192]{1,0:T(4,128)} custom-call(bf16[8,16,384]{2,1,0:T(8,128)(2,1)S(1)} %all-to-all-done.2.got_ref, bf16[128,64]{1,0:T(8,128)(2,1)S(1)} %get-tuple-element.19.chosen_ref, bf16[64,128,128]{2,1,0:T(8,128)(2,1)} %rbf_hbm.3), custom_call_target="tpu_custom_call" | custom-call | tf_op jit(solution)/shard_map/wall/pallas_call | solution.py:536
Async XLA Ops:
  0.6 45.1 %copy-start = (f32[64,32,3,128]{3,1,2,0:T(8,128)S(1)}, f32[64,32,3,128]{3,1,2,0:T(8,128)}, u32[]{:S(2)}) copy-start(f32[64,32,3,128]{3,1,2,0:T(8,128)} %param.22) | copy-start | bytes 9437188
  0.6 39.6 %copy-start.2 = (f32[32,128]{1,0:T(8,128)S(1)}, f32[32,128]{1,0:T(8,128)}, u32[]{:S(2)}) copy-start(f32[32,128]{1,0:T(8,128)} %stiff_ref.3) | copy-start | bytes 49156
  0.7 39.6 %copy-start.1 = (f32[32,3,128]{2,0,1:T(8,128)S(1)}, f32[32,3,128]{2,0,1:T(8,128)}, u32[]{:S(2)}) copy-start(f32[32,3,128]{2,0,1:T(8,128)} %param.20) | copy-start | bytes 147460
  1.5 8.1 %collective-permute-start.1 = (bf16[3,1,128]{2,1,0:T(2,128)(2,1)S(1)}, bf16[3,1,128]{2,1,0:T(2,128)(2,1)S(1)}, u32[]{:S(2)}, u32[]{:S(2)}) collective-permute-start(bf16[3,1,128]{2,1,0:T(2,128)(2,1)S(1)} %get-tuple-element.34), channel_id=1, source_target_pairs={{0,1},{1,2},{2,3},{3,4},{4,5},{5,6},{6,7},{7,8},{8,9},{9,10},{10,1... | collective-permute-start | bytes 2312 | tf_op jit(solution)/shard_map/ppermute | solution.py:587
  4.1 5.6 %collective-permute-start = (bf16[3,1,128]{2,1,0:T(2,128)(2,1)S(1)}, bf16[3,1,128]{2,1,0:T(2,128)(2,1)S(1)}, u32[]{:S(2)}, u32[]{:S(2)}) collective-permute-start(bf16[3,1,128]{2,1,0:T(2,128)(2,1)S(1)} %get-tuple-element.35), channel_id=1, source_target_pairs={{1,0},{2,1},{3,2},{4,3},{5,4},{6,5},{7,6},{8,7},{9,8},{10,9},{11,1... | collective-permute-start | bytes 2312 | tf_op jit(solution)/shard_map/ppermute | solution.py:588
  40.5 2.6 %collective-permute-start.2 = (f32[24,128]{1,0:T(8,128)S(1)}, f32[24,128]{1,0:T(8,128)S(1)}, u32[]{:S(2)}, u32[]{:S(2)}) collective-permute-start(f32[24,128]{1,0:T(8,128)S(1)} %get-tuple-element.25), channel_id=1, source_target_pairs={{0,1},{1,2},{2,3},{3,4},{4,5},{5,6},{6,7},{7,8},{8,9},{9,10},{10,1... | collective-permute-start | bytes 36872 | tf_op jit(solution)/shard_map/ppermute | solution.py:597
  41.8 3.9 %collective-permute-start.3 = (f32[24,128]{1,0:T(8,128)S(1)}, f32[24,128]{1,0:T(8,128)S(1)}, u32[]{:S(2)}, u32[]{:S(2)}) collective-permute-start(f32[24,128]{1,0:T(8,128)S(1)} %get-tuple-element.26), channel_id=1, source_target_pairs={{1,0},{2,1},{3,2},{4,3},{5,4},{6,5},{7,6},{8,7},{9,8},{10,9},{11,1... | collective-permute-start | bytes 36872 | tf_op jit(solution)/shard_map/ppermute | solution.py:598
  64.1 10.5 %all-to-all-start.2 = ((bf16[8,16,384]{2,1,0:T(8,128)(2,1)}), bf16[8,16,384]{2,1,0:T(8,128)(2,1)S(1)}, u32[]{:S(2)}, u32[]{:S(2)}) async-start(bf16[8,16,384]{2,1,0:T(8,128)(2,1)} %get-tuple-element.32), calls=%async_computation.2 | async-start | bytes 196608 | tf_op jit(solution)/shard_map/all_to_all | solution.py:603
